TPU v7x, 16 devices: a whole 2x2x2 slice. The times are simulated.
16 devices in a mesh: sweep: 2 (over z), ent: 8 (over y, x, core).
Axes of the slice: x: 2, y: 2, z: 2, core: 2. Of those that a mesh axis runs over, the one named last changes fastest.
Arguments:
- ent_table: float32 [262144, 400], P(('sweep', 'ent')), parts along dimension 0
- ada_state: float32 [262144], P(('sweep', 'ent')), parts along dimension 0
- rel_table: float32 [2690, 400], P('sweep'), parts along dimension 0
- head_idx: int32 [16, 6, 1024], P(('sweep', 'ent')), parts along dimension 0
- tail_idx: int32 [16, 6, 1024], P(('sweep', 'ent')), parts along dimension 0
- rel_idx: int32 [16, 6, 1024], P(('sweep', 'ent')), parts along dimension 0
- neg_idx: int32 [16, 6, 1024], P(('sweep', 'ent')), parts along dimension 0
- edge_mask: int32 [16, 6, 1024], P(('sweep', 'ent')), parts along dimension 0
Outputs:
- output 1: float32 [262144, 400], P(('sweep', 'ent')), parts along dimension 0
- output 2: float32 [262144], P(('sweep', 'ent')), parts along dimension 0
- output 3: float32 [2690, 400], P('sweep'), parts along dimension 0
- output 4: float32 [16, 6], P(('sweep', 'ent')), parts along dimension 0
There are 2 independent parts. A program takes and returns all parts, laid end to end along the dimension named above; each array names one.
All inputs are finite; a program needn't handle non-finite values.
Results may differ from a plain program's by a relative error of at most 0.00243552.
Values are sent between devices in bfloat16 or wider.
A program may use at most 1 GiB of HBM per device.

v0:
```python
import functools

import jax
import jax.numpy as jnp
from jax import lax
from jax.experimental import pallas as pl
from jax.experimental.pallas import tpu as pltpu
from jax.sharding import PartitionSpec as P


LEARN_RATE = 0.25
ADA_EPS = 1e-10

DIM = 400
HALF = 200
ACC_LANE = 16
LANES = 128
MIB = 1 << 20
GRANT = 7
TAILS_FIRST = (True, False)

VM = pl.BlockSpec(memory_space=pltpu.VMEM)
SM = pl.BlockSpec(memory_space=pltpu.SMEM)
HBM = pl.BlockSpec(memory_space=pltpu.HBM)
F32 = jnp.float32
BF16 = jnp.bfloat16


def params(mib):
    return pltpu.CompilerParams(vmem_limit_bytes=mib * MIB)


def lane_ids(shape):
    return lax.broadcasted_iota(jnp.int32, shape, 1)


def swap_two(x):
    return pltpu.roll(x, 64, 1)


def swap_three(x):
    return jnp.where(lane_ids(x.shape) < 8, pltpu.roll(x, 120, 1), pltpu.roll(x, 8, 1))


def times(a, b):
    out = [a[0] * b[0] - a[1] * b[1], a[0] * b[1] + a[1] * b[0]]
    for x, y, swap, edge in ((a[2], b[2], swap_two, 64), (a[3], b[3], swap_three, 8)):
        xs, ys = swap(x), swap(y)
        out.append(jnp.where(lane_ids(x.shape) < edge, x * y - xs * ys, xs * y + x * ys))
    return out


def times_conj(a, b):
    out = [a[0] * b[0] + a[1] * b[1], a[1] * b[0] - a[0] * b[1]]
    for x, y, swap, edge in ((a[2], b[2], swap_two, 64), (a[3], b[3], swap_three, 8)):
        xs, ys = swap(x), swap(y)
        out.append(jnp.where(lane_ids(x.shape) < edge, x * y + xs * ys, x * ys - xs * y))
    return out


def keep_data(x):
    return jnp.where(lane_ids(x.shape) < ACC_LANE, x, 0.0)


def flat(ref):
    return ref.reshape(ref.shape[0] * 4, LANES)


def plane(ref2, start, rows, part):
    return ref2[pl.ds(start * 4 + part, rows, stride=4), :]


def put_plane(ref2, start, rows, part, x):
    ref2[pl.ds(start * 4 + part, rows, stride=4), :] = x


def copy_rows(idx_ref, count, src, dst, offset):
    def body(i, carry):
        dst[offset + i] = src[idx_ref[i]]
        return carry

    lax.fori_loop(0, count, body, 0, unroll=16)


def pack_rows(dst, src2, rows, first, groups, packed):
    step = rows // 8
    for g in range(groups):
        at, to = g * step, (first + g) * step
        for part in range(3):
            dst[part * rows + to:part * rows + to + step, :] = plane(src2, at, step, part).astype(dst.dtype)
        last = keep_data(plane(src2, at, step, 3))
        if first + g:
            last = pltpu.roll(last, 16 * (first + g), 1)
        packed = last if packed is None else packed + last
    if first + groups == 8:
        dst[3 * rows:3 * rows + step, :] = packed.astype(dst.dtype)
    return packed


def unpack_part(src, rows, g, step):
    planes = [src[part * rows + g * step:part * rows + (g + 1) * step, :].astype(F32) for part in range(3)]
    last = src[3 * rows:3 * rows + step, :].astype(F32)
    if g:
        last = pltpu.roll(last, LANES - 16 * g, 1)
    planes.append(keep_data(last))
    return planes


def row_parts(ent_ref, state, cols):
    return [
        ent_ref[0:128, :],
        ent_ref[HALF:HALF + 128, :],
        jnp.concatenate([ent_ref[128:192, :], ent_ref[HALF + 128:HALF + 192, :]], axis=0),
        jnp.concatenate([ent_ref[192:200, :], ent_ref[HALF + 192:HALF + 200, :], state, jnp.zeros((104, cols), F32)], axis=0),
    ]


def put_columns(ent_ref, x, part):
    if part < 2:
        ent_ref[part * HALF:part * HALF + 128, :] = x
    elif part == 2:
        ent_ref[128:192, :] = x[0:64]
        ent_ref[HALF + 128:HALF + 192, :] = x[64:128]
    else:
        ent_ref[192:200, :] = x[0:8]
        ent_ref[HALF + 192:HALF + 200, :] = x[8:16]


def load_kernel(ent_hbm, tab_ref, hold_ref, sems):
    cols = hold_ref.shape[2]
    blocks = ent_hbm.shape[1] // cols
    tab2 = flat(tab_ref)

    def fetch(b, slot):
        return pltpu.make_async_copy(ent_hbm.at[:, pl.ds(pl.multiple_of(b * cols, cols), cols)], hold_ref.at[slot], sems.at[slot])

    slots = hold_ref.shape[0]
    for b in range(slots - 1):
        fetch(b, b).start()

    def body(b, carry):
        slot = lax.rem(b, slots)
        fetch(b, slot).wait()
        ahead = b + slots - 1

        @pl.when(ahead < blocks)
        def _():
            fetch(ahead, lax.rem(ahead, slots)).start()

        parts = row_parts(hold_ref.at[slot], jnp.zeros((8, cols), F32), cols)
        for part in range(4):
            tab2[pl.ds(b * (cols * 4) + part, cols, stride=4), :] = parts[part].T
        return carry

    lax.fori_loop(0, blocks, body, 0)


def load_rel_kernel(rel_ref, ada_ref, tab_ref, *, areas):
    tab2 = flat(tab_ref)
    block = 512

    def body(b, carry):
        state = jnp.broadcast_to(ada_ref[:, pl.ds(pl.multiple_of(b * block, block), block)], (LANES, block)).T
        at = pl.ds(b * (block * 4) + 3, block, stride=4)
        tab2[at, :] = jnp.where(lane_ids(state.shape) == ACC_LANE, state, tab2[at, :])
        return carry

    lax.fori_loop(0, ada_ref.shape[1] // block, body, 0)
    base, rows = areas['rel']
    count = rel_ref.shape[1]
    parts = row_parts(rel_ref, jnp.zeros((8, count), F32), count)
    for part in range(4):
        tab2[pl.ds(4 * base + part, count, stride=4), :] = parts[part].T
    tab_ref[base + count:base + rows] = jnp.zeros((rows - count, 4, LANES), F32)


def store_kernel(tab_ref, ent_ref, ada_ref):
    cols = ent_ref.shape[1]
    tab2 = flat(tab_ref)
    start = pl.program_id(0) * (cols * 4)
    for part in range(4):
        x = tab2[pl.ds(start + part, cols, stride=4), :].T
        put_columns(ent_ref, x, part)
        if part == 3:
            ada_ref[...] = x[ACC_LANE:ACC_LANE + 1]


def store_rel_kernel(tab_ref, rel_ref, loss_ref, *, areas, edges):
    tab2 = flat(tab_ref)
    count = rel_ref.shape[1]
    for part in range(4):
        put_columns(rel_ref, tab2[pl.ds(4 * areas['rel'][0] + part, count, stride=4), :].T, part)
    base, rounds = areas['loss']
    lane = lane_ids((1, LANES))
    total = jnp.zeros((1, LANES), F32)
    for step in range(rounds):
        total = jnp.where(lane == step, tab2[4 * (base + step):4 * (base + step) + 1, :], total)
    loss_ref[...] = total * (1.0 / edges)


def gather_tails_kernel(tail_ref, neg_ref, tail_out, tab_ref, hold_ref, *, areas):
    edges = tail_ref.shape[0]
    hold2 = flat(hold_ref)
    copy_rows(tail_ref, edges, tab_ref, hold_ref, 0)
    packed = pack_rows(tail_out, hold2, 2 * edges, 0, 4, None)
    copy_rows(neg_ref, edges, tab_ref, hold_ref, 0)
    pack_rows(tail_out, hold2, 2 * edges, 4, 4, packed)


def gather_heads_kernel(head_ref, one_out, two_out, tab_ref, hold_ref, *, areas):
    edges = head_ref.shape[0]
    copy_rows(head_ref, edges, tab_ref, hold_ref, 0)
    for side, out in enumerate((one_out, two_out)):
        half = hold_ref.at[pl.ds(side * (edges // 2), edges // 2)]
        pack_rows(out, flat(half), edges // 2, 0, 8, None)


def adagrad(grad, row):
    total = grad[0] * grad[0] + grad[1] * grad[1] + grad[2] * grad[2] + grad[3] * grad[3]
    mean = jnp.sum(total, axis=1, keepdims=True) * (1.0 / DIM)
    lane = lane_ids(row[3].shape)
    state = jnp.sum(jnp.where(lane == ACC_LANE, row[3], 0.0), axis=1, keepdims=True) + mean
    rate = LEARN_RATE / jnp.sqrt(state + ADA_EPS)
    new = [row[part] - grad[part] * rate for part in range(4)]
    new[3] = jnp.where(lane == ACC_LANE, state, new[3])
    return new


def apply_rows(key_ref, grad_ref, tab_ref, sum_ref, row_ref):
    size = sum_ref.shape[0]
    sum2, row2 = flat(sum_ref), flat(row_ref)
    block = 128

    def chunk(c, carry):
        base = c * size

        def collect(e, carry):
            prev, acc, old = carry
            key = key_ref[base + e]
            row = key >> 12
            same = row == prev
            g = grad_ref[key & 4095]
            acc = jnp.where(same, acc + g, g)
            old = jnp.where(same, old, tab_ref[row])
            sum_ref[e] = acc
            row_ref[e] = old
            return row, acc, old

        carry = lax.fori_loop(0, size, collect, carry, unroll=16)

        def update(b, carry):
            at = b * (block * 4)
            grad = [sum2[pl.ds(at + part, block, stride=4), :] for part in range(4)]
            row = [row2[pl.ds(at + part, block, stride=4), :] for part in range(4)]
            new = adagrad(grad, row)
            for part in range(4):
                row2[pl.ds(at + part, block, stride=4), :] = new[part]
            return carry

        lax.fori_loop(0, size // block, update, 0)

        def write(e, carry):
            tab_ref[key_ref[base + e] >> 12] = row_ref[e]
            return carry

        lax.fori_loop(0, size, write, 0, unroll=16)
        return carry

    zero = jnp.zeros((4, LANES), F32)
    lax.fori_loop(0, key_ref.shape[0] // size, chunk, (jnp.int32(-1), zero, zero))


def update_kernel(key_ref, tab_ref, sum_ref, row_ref, *, areas):
    apply_rows(key_ref, tab_ref.at[pl.ds(*areas['grad'])], tab_ref, sum_ref, row_ref)


def put_wide(ref, start, rows, planes):
    for part in range(4):
        ref[start:start + rows, part * LANES:(part + 1) * LANES] = planes[part].astype(ref.dtype)


def unpack_negs(tail_ref, neg_ref):
    edges = neg_ref.shape[0]
    wide = edges // 4
    for g in range(4):
        put_wide(neg_ref, g * wide, wide, unpack_part(tail_ref, 2 * edges, g + 4, wide))


def put_queries(head_ref, hold2, query_ref, start):
    rows = head_ref.shape[0] * 8 // 25
    step = rows // 8
    for g in range(8):
        heads = unpack_part(head_ref, rows, g, step)
        rels = [plane(hold2, start + g * step, step, part) for part in range(4)]
        rels[3] = keep_data(rels[3])
        put_wide(query_ref, start + g * step, step, times(heads, rels))


def tail_block(tail_ref, b, block):
    rows = 8 * block
    planes = [tail_ref[pl.ds(pl.multiple_of(part * rows + b * block, block), block), :].astype(F32) for part in range(3)]
    last = tail_ref[3 * rows:3 * rows + block, :].astype(F32)
    planes.append(keep_data(pltpu.roll(last, LANES - 16 * b, 1)))
    return planes


def head_kernel(rel_ref, key_ref, weight_ref, one_ref, two_ref, tail_ref, give_out, tab_ref, query_ref, neg_ref, *, areas, step_no):
    rel_tab, grad_out = tab_ref.at[pl.ds(*areas['rel'])], tab_ref.at[pl.ds(*areas['grad'])]
    edges = rel_ref.shape[0]
    hold_ref = grad_out.at[pl.ds(edges, edges)]
    copy_rows(rel_ref, edges, rel_tab, hold_ref, 0)
    unpack_negs(tail_ref, neg_ref)
    scale = DIM ** -0.5
    for side, head_ref in enumerate((one_ref, two_ref)):
        put_queries(head_ref, flat(hold_ref), query_ref, side * (edges // 2))
    block = edges // 4

    def body(b, loss):
        at = pl.ds(pl.multiple_of(b * block, block), block)
        query = query_ref[at, :]
        tails = jnp.concatenate(tail_block(tail_ref, b, block), axis=1)
        pos = scale * jnp.sum(query * tails, axis=1, keepdims=True)
        neg = scale * lax.dot_general(query.astype(BF16), neg_ref[...], (((1,), (1,)), ((), ())), preferred_element_type=F32)
        top = jnp.maximum(pos, jnp.max(neg, axis=1, keepdims=True))
        pos_exp = jnp.exp(pos - top)
        neg_exp = jnp.exp(neg - top)
        denom = pos_exp + jnp.sum(neg_exp, axis=1, keepdims=True)
        weight = weight_ref[at, step_no:step_no + 1]
        loss = loss + weight * (top + jnp.log(denom) - pos)
        d_pos = weight * (pos_exp / denom - 1.0)
        d_neg = ((weight / denom) * neg_exp).astype(BF16)
        query_ref[at, :] = scale * (d_pos * tails + jnp.dot(d_neg, neg_ref[...], preferred_element_type=F32))
        return loss

    loss = lax.fori_loop(0, edges // block, body, jnp.zeros((block, 1), F32))
    tab_ref[areas['loss'][0] + step_no] = jnp.broadcast_to(jnp.sum(loss, axis=0, keepdims=True), (4, LANES))
    hold2, grad2 = flat(hold_ref), flat(grad_out)
    half = edges // 2
    step = half // 8
    for side, head_ref in enumerate((one_ref, two_ref)):
        for g in range(8):
            at = side * half + g * step
            heads = unpack_part(head_ref, half, g, step)
            rels = [plane(hold2, at, step, part) for part in range(4)]
            rels[3] = keep_data(rels[3])
            d_query = [query_ref[at:at + step, part * LANES:(part + 1) * LANES] for part in range(4)]
            d_head = times_conj(d_query, rels)
            d_rel = times_conj(d_query, heads)
            for part in range(4):
                put_plane(grad2, at, step, part, d_head[part])
                put_plane(hold2, at, step, part, d_rel[part])

    rel_rows = rel_tab.shape[0]
    sum_ref = grad_out.at[pl.ds(2 * edges, rel_rows)]
    sum_ref[...] = jnp.zeros(sum_ref.shape, F32)

    def scatter(e, carry):
        prev, acc = carry
        key = key_ref[e]
        row = key >> 10
        g = hold_ref[key & 1023]
        acc = jnp.where(row == prev, acc + g, g)
        sum_ref[row] = acc
        return row, acc

    lax.fori_loop(0, edges, scatter, (jnp.int32(-1), jnp.zeros((4, LANES), F32)), unroll=16)
    drel_out = flat(tab_ref.at[pl.ds(*areas['drel'])])
    pack_rows(drel_out, flat(sum_ref), rel_rows, 0, 8, None)
    used, half = rel_rows * 25 // 8, give_out.shape[0]
    drel_out[used:, :] = jnp.zeros((2 * half - used, LANES), F32)
    core = lax.rem(lax.axis_index('ent'), 2)
    give_out[...] = drel_out[pl.ds(pl.multiple_of((1 - core) * half, 8), half), :]


def tail_kernel(rel_ref, weight_ref, head_ref, tail_ref, tab_ref, query_ref, neg_ref, sum_ref, *, areas, side, last):
    rel_tab, grad_out = tab_ref.at[pl.ds(*areas['rel'])], tab_ref.at[pl.ds(*areas['grad'])]
    edges = neg_ref.shape[0]
    half = edges // 2
    hold_ref = grad_out.at[pl.ds(edges + side * half, half)]
    unpack_negs(tail_ref, neg_ref)

    def fetch(i, carry):
        hold_ref[i] = rel_tab[rel_ref[side * half + i]]
        return carry

    lax.fori_loop(0, half, fetch, 0, unroll=16)
    put_queries(head_ref, flat(hold_ref), query_ref, 0)
    scale = DIM ** -0.5
    block = edges // 4
    grad2 = flat(grad_out)
    sum_ref[...] = jnp.zeros(sum_ref.shape, F32)

    def body(b, carry):
        at = pl.ds(pl.multiple_of(b * block, block), block)
        query = query_ref[at, :]
        query_bf = query.astype(BF16)
        tails = tail_block(tail_ref, b + 2 * side, block)
        prod = [query[:, part * LANES:(part + 1) * LANES] * tails[part] for part in range(4)]
        prod = (prod[0] + prod[1]) + (prod[2] + prod[3])
        pos = scale * jnp.sum(prod.T, axis=0, keepdims=True)
        neg = scale * lax.dot_general(neg_ref[...], query_bf, (((1,), (1,)), ((), ())), preferred_element_type=F32)
        top = jnp.maximum(pos, jnp.max(neg, axis=0, keepdims=True))
        pos_exp = jnp.exp(pos - top)
        neg_exp = jnp.exp(neg - top)
        denom = pos_exp + jnp.sum(neg_exp, axis=0, keepdims=True)
        weight = weight_ref[pl.ds(b + 2 * side, 1), :]
        d_pos = weight * (pos_exp / denom - 1.0)
        d_neg = ((weight / denom) * neg_exp).astype(BF16)
        sum_ref[...] += jnp.dot(d_neg, query_bf, preferred_element_type=F32)
        d_pos_col = jnp.broadcast_to(d_pos, (LANES, block)).T
        for part in range(4):
            grad2[pl.ds((edges + side * half + b * block) * 4 + part, block, stride=4), :] = scale * d_pos_col * query[:, part * LANES:(part + 1) * LANES]
        return carry

    lax.fori_loop(0, half // block, body, 0)
    for part in range(4):
        total = scale * sum_ref[:, part * LANES:(part + 1) * LANES]
        if last:
            total = total + plane(grad2, 2 * edges, edges, part)
        put_plane(grad2, 2 * edges, edges, part, total)


def split_kernel(got_ref, own_out, one_out, two_out, three_out, tab_ref, *, areas):
    drel_ref = flat(tab_ref.at[pl.ds(*areas['drel'])])
    half, piece = got_ref.shape[0], own_out.shape[0]
    me = lax.axis_index('ent')
    core, chip = lax.rem(me, 2), lax.div(me, 2)
    for away, out in enumerate((own_out, one_out, two_out, three_out)):
        at = pl.multiple_of((chip ^ away) * piece, 8)
        out[...] = drel_ref[pl.ds(pl.multiple_of(core * half + at, 8), piece), :] + got_ref[pl.ds(at, piece), :]


def sum_kernel(own_ref, one_ref, two_ref, three_ref, out, tab_ref, *, areas):
    out[...] = (own_ref[...] + one_ref[...]) + (two_ref[...] + three_ref[...])


def join_kernel(own_ref, one_ref, two_ref, three_ref, out, tab_ref, *, areas):
    piece = own_ref.shape[0]
    chip = lax.div(lax.axis_index('ent'), 2)
    for away, ref in enumerate((own_ref, one_ref, two_ref, three_ref)):
        out[pl.ds(pl.multiple_of((chip ^ away) * piece, 8), piece), :] = ref[...]


def rel_kernel(half_ref, far_ref, tab_ref, *, areas):
    drel_ref = flat(tab_ref.at[pl.ds(*areas['drel'])])
    rel_tab = tab_ref.at[pl.ds(*areas['rel'])]
    rows = rel_tab.shape[0]
    half = half_ref.shape[0]
    core = lax.rem(lax.axis_index('ent'), 2)
    drel_ref[pl.ds(pl.multiple_of(core * half, 8), half), :] = half_ref[...]
    drel_ref[pl.ds(pl.multiple_of((1 - core) * half, 8), half), :] = far_ref[...]
    step = rows // 8
    rel2 = flat(rel_tab)
    for g in range(8):
        grad = unpack_part(drel_ref, rows, g, step)
        row = [plane(rel2, g * step, step, part) for part in range(4)]
        new = adagrad(grad, row)
        for part in range(4):
            put_plane(rel2, g * step, step, part, new[part])


def shape(*dims, dtype=F32):
    return jax.ShapeDtypeStruct(dims, dtype)


def solution(mesh):
    ent_devs = mesh.shape['ent']
    row_spec = P(('sweep', 'ent'), None)
    state_spec = P(('sweep', 'ent'))
    rel_spec = P('sweep', None)
    edge_spec = P(('sweep', 'ent'), None, None)

    def train(ent_part, ada_part, rel_table, head_idx, tail_idx, rel_idx, neg_idx, edge_mask):
        part_rows = ent_part.shape[0]
        rel_count = rel_table.shape[0]
        rounds = head_idx.shape[1]
        edges = head_idx.shape[2]
        rel_rows = -(-rel_count // 128) * 128
        head_idx, tail_idx, rel_idx, neg_idx, edge_mask = (x[0] for x in (head_idx, tail_idx, rel_idx, neg_idx, edge_mask))

        piece = -(-(rel_rows * 25 // 8) // 64) * 8

        def away(bits):
            return [(sender, sender ^ bits) for sender in range(ent_devs)]

        def ring(step):
            shift = step + 1
            to_owner = [(sender, (sender + shift) % ent_devs) for sender in range(ent_devs)]
            return to_owner, [(target, sender) for sender, target in to_owner]

        asked = jnp.stack([tail_idx, neg_idx, rel_idx, edge_mask], axis=1)
        served = jnp.stack([lax.ppermute(asked[step], 'ent', ring(step)[0]) for step in range(rounds)])
        rows_all = jnp.concatenate([head_idx, served[:, 0], served[:, 1]], axis=1)
        keys = lax.sort(rows_all * 4096 + jnp.arange(3 * edges, dtype=jnp.int32)[None, :], dimension=1, is_stable=False)
        rel_keys = lax.sort(rel_idx * 1024 + jnp.arange(edges, dtype=jnp.int32)[None, :], dimension=1, is_stable=False)
        own_weight = jnp.pad(edge_mask.astype(F32), ((0, 8 - rounds), (0, 0))).T
        serve_weight = served[:, 3].astype(F32).reshape(rounds, edges // 256, 256)
        small = []
        for step in range(rounds):
            small.append((head_idx[step], served[step, 0], served[step, 1], served[step, 2], rel_idx[step], keys[step], rel_keys[step], serve_weight[step]))
        small, own_weight, rel_cols, ent_cols, ada_row = lax.optimization_barrier((small, own_weight, rel_table.T, ent_part.T, ada_part.reshape(1, part_rows)))

        cols = 512
        grad_rows = 2 * edges + max(edges, rel_rows)
        areas = {'grad': (part_rows, grad_rows), 'rel': (part_rows + grad_rows, rel_rows), 'drel': (part_rows + grad_rows + rel_rows, 2 * piece)}
        areas['loss'] = (sum(areas['drel']), rounds)
        tab_shape = pltpu.VMEM((sum(areas['loss']), 4, LANES), F32)
        head_wire, tail_wire = shape(edges * 25 // 16, LANES), shape(2 * edges * 25 // 8, LANES, dtype=BF16)
        part_wire, half_wire = shape(piece, LANES), shape(4 * piece, LANES)
        hold = pltpu.VMEM((edges, 4, LANES), F32)
        work = [pltpu.VMEM((edges, 512), F32), pltpu.VMEM((edges, 512), BF16)]

        def call(kernel, tab, inputs, in_specs, out_shape, out_specs, scratch=(), **more):
            ins, outs = len(inputs), len(out_shape)

            def body(*refs):
                kernel(*refs[:ins], *refs[ins + 2:ins + 2 + outs], refs[ins + 1], *refs[ins + 2 + outs:], areas=areas, **more)

            got = pl.pallas_call(
                body, in_specs=in_specs + [VM], out_specs=[VM] + out_specs, out_shape=[tab_shape] + out_shape,
                input_output_aliases={ins: 0}, scratch_shapes=list(scratch), compiler_params=params(GRANT))(*inputs, tab)
            return got[0], got[1:]

        tab = pl.pallas_call(
            load_kernel, in_specs=[HBM], out_specs=VM, out_shape=tab_shape,
            scratch_shapes=[pltpu.VMEM((4, DIM, cols), F32), pltpu.SemaphoreType.DMA((4,))],
            compiler_params=params(GRANT), name="load")(ent_cols)
        tab, _ = call(load_rel_kernel, tab, [rel_cols, ada_row], [VM, VM], [], [])
        half = None
        for step in range(rounds):
            to_owner, to_asker = ring(step)
            head_ids, serve_tails, serve_negs, serve_rel, own_rel, key, rel_key, weight = small[step]
            tab, (tails,) = call(gather_tails_kernel, tab, [serve_tails, serve_negs], [SM] * 2, [tail_wire], [VM], [hold])
            far_tails = lax.ppermute(tails, 'ent', to_asker)
            tab, heads = call(gather_heads_kernel, tab, [head_ids], [SM], [head_wire] * 2, [VM] * 2, [hold])
            if TAILS_FIRST[step % len(TAILS_FIRST)]:
                far_tails, *heads = lax.optimization_barrier((far_tails, *heads))
            far_heads = []
            for side in range(2):
                far_heads.append(lax.ppermute(heads[side], 'ent', to_owner))
            if step:
                tab, _ = call(rel_kernel, tab, [half, far_half], [VM] * 2, [], [])

            def tail_role(tab, side, last):
                return call(
                    tail_kernel, tab, [serve_rel, weight, far_heads[side], tails], [SM, VM, VM, VM], [], [],
                    [pltpu.VMEM((edges // 2, 512), F32), pltpu.VMEM((edges, 512), BF16), pltpu.VMEM((edges, 512), F32)], side=side, last=last)[0]

            tab, (give,) = call(
                head_kernel, tab, [own_rel, rel_key, own_weight, *heads, far_tails], [SM, SM, VM, VM, VM, VM],
                [half_wire], [VM], work, step_no=step)
            got = lax.ppermute(give, 'ent', away(1))
            tab, (own, *parts) = call(split_kernel, tab, [got], [VM], [part_wire] * 4, [VM] * 4)
            parts = [lax.ppermute(x, 'ent', away(2 * hop + 2)) for hop, x in enumerate(parts)]
            tab = tail_role(tab, 0, False)
            tab = tail_role(tab, 1, True)
            tab, (total,) = call(sum_kernel, tab, [own, *parts], [VM] * 4, [part_wire], [VM])
            totals = [lax.ppermute(total, 'ent', away(2 * hop + 2)) for hop in range(3)]
            tab, _ = call(update_kernel, tab, [key], [SM], [], [], [hold, hold])
            tab, (half,) = call(join_kernel, tab, [total, *totals], [VM] * 4, [half_wire], [VM])
            far_half = lax.ppermute(half, 'ent', away(1))
        tab, _ = call(rel_kernel, tab, [half, far_half], [VM] * 2, [], [])

        ent_out, ada_out = pl.pallas_call(
            store_kernel, grid=(part_rows // cols,), in_specs=[VM],
            out_specs=[pl.BlockSpec((DIM, cols), lambda i: (0, i)), pl.BlockSpec((1, cols), lambda i: (0, i))],
            out_shape=[shape(DIM, part_rows), shape(1, part_rows)], compiler_params=params(GRANT), name="store")(tab)
        rel_out, loss_out = pl.pallas_call(
            functools.partial(store_rel_kernel, areas=areas, edges=edges), in_specs=[VM], out_specs=[VM, VM],
            out_shape=[shape(DIM, rel_count), shape(1, LANES)], compiler_params=params(GRANT), name="store_rel")(tab)
        ent_out, ada_out, rel_out, loss_out = lax.optimization_barrier((ent_out, ada_out, rel_out, loss_out))
        return ent_out.T, ada_out.reshape(part_rows), rel_out.T, loss_out[:, :rounds]

    return jax.shard_map(train, mesh=mesh, in_specs=(row_spec, state_spec, rel_spec, edge_spec, edge_spec, edge_spec, edge_spec, edge_spec), out_specs=(row_spec, state_spec, rel_spec, row_spec), check_vma=False)
```

profile of v0, /device:TPU:0, one launch (start us, length us, event | category | flops | bytes accessed | tf_op | source)
XLA Modules:
  0.0 865.2 jit_solution(13514652658950581538)
XLA Ops:
  25.3 10.9 %sort.17.cloned.1.call-done = s32[6,3072]{1,0:T(8,128)} async-done(((s32[6,3072]{1,0:T(8,128)}), s32[6,3072]{1,0:T(8,128)}) %sort.17.cloned.1.call-update) | async-done | bytes 73744 | tf_op jit(solution)/shard_map/sort | solution.py:494
  37.5 14.5 %load.1.refs_2_ = f32[22358,4,128]{2,1,0:T(4,128)S(1)} custom-call(f32[400,16384]{1,0:T(8,128)} %bitcast.140), custom_call_target="tpu_custom_call" | custom-call | tf_op jit(solution)/shard_map/load/pallas_call | solution.py:524
  52.0 5.1 shard_map.111.refs_2_
  65.9 16.4 %collective-permute-done.6.refs_5_ = bf16[6400,128]{1,0:T(8,128)(2,1)S(1)} collective-permute-done((bf16[6400,128]{1,0:T(8,128)(2,1)S(1)}, bf16[6400,128]{1,0:T(8,128)(2,1)S(1)}, u32[]{:S(2)}, u32[]{:S(2)}) %collective-permute-start.6) | collective-permute-done | bytes 1638432 | tf_op jit(solution)/shard_map/ppermute | solution.py:534
  83.5 18.1 %shard_map.114 = (f32[22358,4,128]{2,1,0:T(4,128)S(1)}, f32[2208,128]{1,0:T(8,128)S(1)}) custom-call(s32[1024]{0:T(1024)S(1)} %bitcast.138, s32[1024]{0:T(1024)S(1)} %bitcast.139, f32[1024,8]{1,0:T(8,128)S(1)} %pad_bitcast_fusion.refs_2_, f32[1600,128]{1,0:T(8,128)S(1)} %get-tuple-element.205.refs_3_, ...), custom_call_target="tpu_custom_call", output_to_operand_aliasing={{0}: (6, {})} | custom-call | tf_op jit(solution)/shard_map/pallas_call | solution.py:519
  108.2 12.2 %collective-permute-done.12.refs_2_ = f32[1600,128]{1,0:T(8,128)S(1)} collective-permute-done((f32[1600,128]{1,0:T(8,128)S(1)}, f32[1600,128]{1,0:T(8,128)S(1)}, u32[]{:S(2)}, u32[]{:S(2)}) %collective-permute-start.12) | collective-permute-done | bytes 819232 | tf_op jit(solution)/shard_map/ppermute | solution.py:540
  120.5 7.3 shard_map.116.refs_4_
  129.7 7.2 shard_map.117.refs_4_
  140.5 21.3 %shard_map.119.refs_4_ = f32[22358,4,128]{2,1,0:T(4,128)S(1)} custom-call(s32[3072]{0:T(1024)S(1)} %bitcast.97, f32[22358,4,128]{2,1,0:T(4,128)S(1)} %get-tuple-element.220.refs_1_), custom_call_target="tpu_custom_call", output_to_operand_aliasing={{}: (1, {})} | custom-call | tf_op jit(solution)/shard_map/pallas_call | solution.py:519
  172.0 29.6 %collective-permute-done.16.refs_5_ = bf16[6400,128]{1,0:T(8,128)(2,1)S(1)} collective-permute-done((bf16[6400,128]{1,0:T(8,128)(2,1)S(1)}, bf16[6400,128]{1,0:T(8,128)(2,1)S(1)}, u32[]{:S(2)}, u32[]{:S(2)}) %collective-permute-start.16) | collective-permute-done | bytes 1638432 | tf_op jit(solution)/shard_map/ppermute | solution.py:534
  202.8 18.1 %shard_map.124 = (f32[22358,4,128]{2,1,0:T(4,128)S(1)}, f32[2208,128]{1,0:T(8,128)S(1)}) custom-call(s32[1024]{0:T(1024)S(1)} %bitcast.136, s32[1024]{0:T(1024)S(1)} %bitcast.137, f32[1024,8]{1,0:T(8,128)S(1)} %pad_bitcast_fusion.refs_2_, f32[1600,128]{1,0:T(8,128)S(1)} %get-tuple-element.223.refs_3_, ...), custom_call_target="tpu_custom_call", output_to_operand_aliasing={{0}: (6, {})} | custom-call | tf_op jit(solution)/shard_map/pallas_call | solution.py:519
  227.7 15.4 %collective-permute-done.23.refs_2_ = f32[1600,128]{1,0:T(8,128)S(1)} collective-permute-done((f32[1600,128]{1,0:T(8,128)S(1)}, f32[1600,128]{1,0:T(8,128)S(1)}, u32[]{:S(2)}, u32[]{:S(2)}) %collective-permute-start.23) | collective-permute-done | bytes 819232 | tf_op jit(solution)/shard_map/ppermute | solution.py:540
  243.1 7.3 shard_map.126.refs_4_
  250.4 10.2 %collective-permute-done.22.refs_2_ = f32[1600,128]{1,0:T(8,128)S(1)} collective-permute-done((f32[1600,128]{1,0:T(8,128)S(1)}, f32[1600,128]{1,0:T(8,128)S(1)}, u32[]{:S(2)}, u32[]{:S(2)}) %collective-permute-start.22) | collective-permute-done | bytes 819232 | tf_op jit(solution)/shard_map/ppermute | solution.py:540
  260.6 7.0 shard_map.127.refs_4_
  267.6 4.6 collective-permute-done.21.refs_3_
  275.8 21.3 %shard_map.129.refs_4_ = f32[22358,4,128]{2,1,0:T(4,128)S(1)} custom-call(s32[3072]{0:T(1024)S(1)} %bitcast.96, f32[22358,4,128]{2,1,0:T(4,128)S(1)} %get-tuple-element.239.refs_1_), custom_call_target="tpu_custom_call", output_to_operand_aliasing={{}: (1, {})} | custom-call | tf_op jit(solution)/shard_map/pallas_call | solution.py:519
  307.2 14.5 %collective-permute-done.27.refs_5_ = bf16[6400,128]{1,0:T(8,128)(2,1)S(1)} collective-permute-done((bf16[6400,128]{1,0:T(8,128)(2,1)S(1)}, bf16[6400,128]{1,0:T(8,128)(2,1)S(1)}, u32[]{:S(2)}, u32[]{:S(2)}) %collective-permute-start.27) | collective-permute-done | bytes 1638432 | tf_op jit(solution)/shard_map/ppermute | solution.py:534
  322.9 18.1 %shard_map.134 = (f32[22358,4,128]{2,1,0:T(4,128)S(1)}, f32[2208,128]{1,0:T(8,128)S(1)}) custom-call(s32[1024]{0:T(1024)S(1)} %bitcast.134, s32[1024]{0:T(1024)S(1)} %bitcast.135, f32[1024,8]{1,0:T(8,128)S(1)} %pad_bitcast_fusion.refs_2_, f32[1600,128]{1,0:T(8,128)S(1)} %get-tuple-element.246.refs_3_, ...), custom_call_target="tpu_custom_call", output_to_operand_aliasing={{0}: (6, {})} | custom-call | tf_op jit(solution)/shard_map/pallas_call | solution.py:519
  341.1 17.9 %collective-permute-start.34 = (f32[1600,128]{1,0:T(8,128)S(1)}, f32[1600,128]{1,0:T(8,128)S(1)}, u32[]{:S(2)}, u32[]{:S(2)}) collective-permute-start(f32[1600,128]{1,0:T(8,128)S(1)} %get-tuple-element.246.refs_3_), channel_id=1, source_target_pairs={{0,3},{1,4},{2,5},{3,6},{4,7},{5,0},{6,1},{7,2},{8,11},{9,12},{10,... | collective-permute-start | bytes 2457608 | tf_op jit(solution)/shard_map/ppermute | solution.py:540
  363.7 11.2 %collective-permute-done.34.refs_2_ = f32[1600,128]{1,0:T(8,128)S(1)} collective-permute-done((f32[1600,128]{1,0:T(8,128)S(1)}, f32[1600,128]{1,0:T(8,128)S(1)}, u32[]{:S(2)}, u32[]{:S(2)}) %collective-permute-start.34) | collective-permute-done | bytes 819232 | tf_op jit(solution)/shard_map/ppermute | solution.py:540
  374.9 7.5 shard_map.136.refs_4_
  382.4 14.3 %collective-permute-done.33.refs_2_ = f32[1600,128]{1,0:T(8,128)S(1)} collective-permute-done((f32[1600,128]{1,0:T(8,128)S(1)}, f32[1600,128]{1,0:T(8,128)S(1)}, u32[]{:S(2)}, u32[]{:S(2)}) %collective-permute-start.33) | collective-permute-done | bytes 819232 | tf_op jit(solution)/shard_map/ppermute | solution.py:540
  396.7 6.9 shard_map.137.refs_4_
  407.2 21.3 %shard_map.139.refs_4_ = f32[22358,4,128]{2,1,0:T(4,128)S(1)} custom-call(s32[3072]{0:T(1024)S(1)} %bitcast.95, f32[22358,4,128]{2,1,0:T(4,128)S(1)} %get-tuple-element.262.refs_1_), custom_call_target="tpu_custom_call", output_to_operand_aliasing={{}: (1, {})} | custom-call | tf_op jit(solution)/shard_map/pallas_call | solution.py:519
  438.0 30.1 %collective-permute-done.38.refs_5_ = bf16[6400,128]{1,0:T(8,128)(2,1)S(1)} collective-permute-done((bf16[6400,128]{1,0:T(8,128)(2,1)S(1)}, bf16[6400,128]{1,0:T(8,128)(2,1)S(1)}, u32[]{:S(2)}, u32[]{:S(2)}) %collective-permute-start.38) | collective-permute-done | bytes 1638432 | tf_op jit(solution)/shard_map/ppermute | solution.py:534
  469.3 18.5 %shard_map.144 = (f32[22358,4,128]{2,1,0:T(4,128)S(1)}, f32[2208,128]{1,0:T(8,128)S(1)}) custom-call(s32[1024]{0:T(1024)S(1)} %bitcast.132, s32[1024]{0:T(1024)S(1)} %bitcast.133, f32[1024,8]{1,0:T(8,128)S(1)} %pad_bitcast_fusion.refs_2_, f32[1600,128]{1,0:T(8,128)S(1)} %get-tuple-element.265.refs_3_, ...), custom_call_target="tpu_custom_call", output_to_operand_aliasing={{0}: (6, {})} | custom-call | tf_op jit(solution)/shard_map/pallas_call | solution.py:519
  494.2 20.8 %collective-permute-done.45.refs_2_ = f32[1600,128]{1,0:T(8,128)S(1)} collective-permute-done((f32[1600,128]{1,0:T(8,128)S(1)}, f32[1600,128]{1,0:T(8,128)S(1)}, u32[]{:S(2)}, u32[]{:S(2)}) %collective-permute-start.45) | collective-permute-done | bytes 819232 | tf_op jit(solution)/shard_map/ppermute | solution.py:540
  515.0 7.3 shard_map.146.refs_4_
  522.3 10.3 %collective-permute-done.44.refs_2_ = f32[1600,128]{1,0:T(8,128)S(1)} collective-permute-done((f32[1600,128]{1,0:T(8,128)S(1)}, f32[1600,128]{1,0:T(8,128)S(1)}, u32[]{:S(2)}, u32[]{:S(2)}) %collective-permute-start.44) | collective-permute-done | bytes 819232 | tf_op jit(solution)/shard_map/ppermute | solution.py:540
  532.5 6.9 shard_map.147.refs_4_
  543.0 21.3 %shard_map.149.refs_4_ = f32[22358,4,128]{2,1,0:T(4,128)S(1)} custom-call(s32[3072]{0:T(1024)S(1)} %bitcast.94, f32[22358,4,128]{2,1,0:T(4,128)S(1)} %get-tuple-element.281.refs_1_), custom_call_target="tpu_custom_call", output_to_operand_aliasing={{}: (1, {})} | custom-call | tf_op jit(solution)/shard_map/pallas_call | solution.py:519
  573.6 32.3 %collective-permute-done.49.refs_5_ = bf16[6400,128]{1,0:T(8,128)(2,1)S(1)} collective-permute-done((bf16[6400,128]{1,0:T(8,128)(2,1)S(1)}, bf16[6400,128]{1,0:T(8,128)(2,1)S(1)}, u32[]{:S(2)}, u32[]{:S(2)}) %collective-permute-start.49) | collective-permute-done | bytes 1638432 | tf_op jit(solution)/shard_map/ppermute | solution.py:534
  607.0 18.2 %shard_map.154 = (f32[22358,4,128]{2,1,0:T(4,128)S(1)}, f32[2208,128]{1,0:T(8,128)S(1)}) custom-call(s32[1024]{0:T(1024)S(1)} %bitcast.130, s32[1024]{0:T(1024)S(1)} %bitcast.131, f32[1024,8]{1,0:T(8,128)S(1)} %pad_bitcast_fusion.refs_2_, f32[1600,128]{1,0:T(8,128)S(1)} %get-tuple-element.288.refs_3_, ...), custom_call_target="tpu_custom_call", output_to_operand_aliasing={{0}: (6, {})} | custom-call | tf_op jit(solution)/shard_map/pallas_call | solution.py:519
  631.7 10.6 %collective-permute-done.56.refs_2_ = f32[1600,128]{1,0:T(8,128)S(1)} collective-permute-done((f32[1600,128]{1,0:T(8,128)S(1)}, f32[1600,128]{1,0:T(8,128)S(1)}, u32[]{:S(2)}, u32[]{:S(2)}) %collective-permute-start.56) | collective-permute-done | bytes 819232 | tf_op jit(solution)/shard_map/ppermute | solution.py:540
  642.4 7.3 shard_map.156.refs_4_
  651.9 6.9 shard_map.157.refs_4_
  658.9 11.2 %collective-permute-start.57 = (f32[552,128]{1,0:T(8,128)S(1)}, f32[552,128]{1,0:T(8,128)S(1)}, u32[]{:S(2)}, u32[]{:S(2)}) collective-permute-start(f32[552,128]{1,0:T(8,128)S(1)} %get-tuple-element.302.refs_0_), channel_id=1, source_target_pairs={{0,2},{1,3},{2,0},{3,1},{4,6},{5,7},{6,4},{7,5},{8,10},{9,11},{10,... | collective-permute-start | bytes 847880 | tf_op jit(solution)/shard_map/ppermute | solution.py:558
  671.6 21.3 %shard_map.159.refs_4_ = f32[22358,4,128]{2,1,0:T(4,128)S(1)} custom-call(s32[3072]{0:T(1024)S(1)} %bitcast.93, f32[22358,4,128]{2,1,0:T(4,128)S(1)} %get-tuple-element.304.refs_1_), custom_call_target="tpu_custom_call", output_to_operand_aliasing={{}: (1, {})} | custom-call | tf_op jit(solution)/shard_map/pallas_call | solution.py:519
  703.3 32.9 %collective-permute-done.60.refs_5_ = bf16[6400,128]{1,0:T(8,128)(2,1)S(1)} collective-permute-done((bf16[6400,128]{1,0:T(8,128)(2,1)S(1)}, bf16[6400,128]{1,0:T(8,128)(2,1)S(1)}, u32[]{:S(2)}, u32[]{:S(2)}) %collective-permute-start.60) | collective-permute-done | bytes 1638432 | tf_op jit(solution)/shard_map/ppermute | solution.py:534
  737.4 18.2 %shard_map.164 = (f32[22358,4,128]{2,1,0:T(4,128)S(1)}, f32[2208,128]{1,0:T(8,128)S(1)}) custom-call(s32[1024]{0:T(1024)S(1)} %bitcast.128, s32[1024]{0:T(1024)S(1)} %bitcast.129, f32[1024,8]{1,0:T(8,128)S(1)} %pad_bitcast_fusion.refs_2_, f32[1600,128]{1,0:T(8,128)S(1)} %get-tuple-element.307.refs_3_, ...), custom_call_target="tpu_custom_call", output_to_operand_aliasing={{0}: (6, {})} | custom-call | tf_op jit(solution)/shard_map/pallas_call | solution.py:519
  762.2 14.7 %collective-permute-done.67.refs_2_ = f32[1600,128]{1,0:T(8,128)S(1)} collective-permute-done((f32[1600,128]{1,0:T(8,128)S(1)}, f32[1600,128]{1,0:T(8,128)S(1)}, u32[]{:S(2)}, u32[]{:S(2)}) %collective-permute-start.67) | collective-permute-done | bytes 819232 | tf_op jit(solution)/shard_map/ppermute | solution.py:540
  776.9 7.3 shard_map.166.refs_4_
  784.2 10.3 %collective-permute-done.66.refs_2_ = f32[1600,128]{1,0:T(8,128)S(1)} collective-permute-done((f32[1600,128]{1,0:T(8,128)S(1)}, f32[1600,128]{1,0:T(8,128)S(1)}, u32[]{:S(2)}, u32[]{:S(2)}) %collective-permute-start.66) | collective-permute-done | bytes 819232 | tf_op jit(solution)/shard_map/ppermute | solution.py:540
  794.5 6.9 shard_map.167.refs_4_
  801.4 5.2 collective-permute-done.65.refs_3_
  810.1 21.5 %shard_map.169.refs_4_ = f32[22358,4,128]{2,1,0:T(4,128)S(1)} custom-call(s32[3072]{0:T(1024)S(1)} %bitcast.92, f32[22358,4,128]{2,1,0:T(4,128)S(1)} %get-tuple-element.323.refs_1_), custom_call_target="tpu_custom_call", output_to_operand_aliasing={{}: (1, {})} | custom-call | tf_op jit(solution)/shard_map/pallas_call | solution.py:519
  836.2 19.5 %store.1 = (f32[400,16384]{1,0:T(8,128)}, f32[1,16384]{1,0:T(1,128)}) custom-call(f32[22358,4,128]{2,1,0:T(4,128)S(1)} %shard_map.171.tab_ref), custom_call_target="tpu_custom_call" | custom-call | tf_op jit(solution)/shard_map/store/pallas_call | solution.py:564
  (216 shorter events, 152.3 us)
Async XLA Ops:
  102.2 27.5 %collective-permute-start.11 = (f32[1600,128]{1,0:T(8,128)S(1)}, f32[1600,128]{1,0:T(8,128)S(1)}, u32[]{:S(2)}, u32[]{:S(2)}) collective-permute-start(f32[1600,128]{1,0:T(8,128)S(1)} %get-tuple-element.206.refs_4_), channel_id=1, source_target_pairs={{0,1},{1,2},{2,3},{3,4},{4,5},{5,6},{6,7},{7,0},{8,9},{9,10},{10,1... | collective-permute-start | bytes 2457608 | tf_op jit(solution)/shard_map/ppermute | solution.py:540
  104.7 32.2 %collective-permute-start.10 = (f32[552,128]{1,0:T(8,128)S(1)}, f32[552,128]{1,0:T(8,128)S(1)}, u32[]{:S(2)}, u32[]{:S(2)}) collective-permute-start(f32[552,128]{1,0:T(8,128)S(1)} %get-tuple-element.214), channel_id=1, source_target_pairs={{0,6},{1,7},{2,4},{3,5},{4,2},{5,3},{6,0},{7,1},{8,14},{9,15},{10,... | collective-permute-start | bytes 847880 | tf_op jit(solution)/shard_map/ppermute | solution.py:554
  107.4 29.5 %collective-permute-start.8 = (f32[552,128]{1,0:T(8,128)S(1)}, f32[552,128]{1,0:T(8,128)S(1)}, u32[]{:S(2)}, u32[]{:S(2)}) collective-permute-start(f32[552,128]{1,0:T(8,128)S(1)} %get-tuple-element.212), channel_id=1, source_target_pairs={{0,2},{1,3},{2,0},{3,1},{4,6},{5,7},{6,4},{7,5},{8,10},{9,11},{10,... | collective-permute-start | bytes 847880 | tf_op jit(solution)/shard_map/ppermute | solution.py:554
  107.9 29.0 %collective-permute-start.9 = (f32[552,128]{1,0:T(8,128)S(1)}, f32[552,128]{1,0:T(8,128)S(1)}, u32[]{:S(2)}, u32[]{:S(2)}) collective-permute-start(f32[552,128]{1,0:T(8,128)S(1)} %get-tuple-element.213), channel_id=1, source_target_pairs={{0,4},{1,5},{2,6},{3,7},{4,0},{5,1},{6,2},{7,3},{8,12},{9,13},{10,... | collective-permute-start | bytes 847880 | tf_op jit(solution)/shard_map/ppermute | solution.py:554
  137.0 24.8 %collective-permute-start.13 = (f32[552,128]{1,0:T(8,128)S(1)}, f32[552,128]{1,0:T(8,128)S(1)}, u32[]{:S(2)}, u32[]{:S(2)}) collective-permute-start(f32[552,128]{1,0:T(8,128)S(1)} %get-tuple-element.218.refs_0_), channel_id=1, source_target_pairs={{0,2},{1,3},{2,0},{3,1},{4,6},{5,7},{6,4},{7,5},{8,10},{9,11},{10,... | collective-permute-start | bytes 847880 | tf_op jit(solution)/shard_map/ppermute | solution.py:558
  137.8 24.1 %collective-permute-start.14 = (f32[552,128]{1,0:T(8,128)S(1)}, f32[552,128]{1,0:T(8,128)S(1)}, u32[]{:S(2)}, u32[]{:S(2)}) collective-permute-start(f32[552,128]{1,0:T(8,128)S(1)} %get-tuple-element.218.refs_0_), channel_id=1, source_target_pairs={{0,4},{1,5},{2,6},{3,7},{4,0},{5,1},{6,2},{7,3},{8,12},{9,13},{10,... | collective-permute-start | bytes 847880 | tf_op jit(solution)/shard_map/ppermute | solution.py:558
  139.3 22.6 %collective-permute-start.15 = (f32[552,128]{1,0:T(8,128)S(1)}, f32[552,128]{1,0:T(8,128)S(1)}, u32[]{:S(2)}, u32[]{:S(2)}) collective-permute-start(f32[552,128]{1,0:T(8,128)S(1)} %get-tuple-element.218.refs_0_), channel_id=1, source_target_pairs={{0,6},{1,7},{2,4},{3,5},{4,2},{5,3},{6,0},{7,1},{8,14},{9,15},{10,... | collective-permute-start | bytes 847880 | tf_op jit(solution)/shard_map/ppermute | solution.py:558
  165.9 35.8 %collective-permute-start.16 = (bf16[6400,128]{1,0:T(8,128)(2,1)S(1)}, bf16[6400,128]{1,0:T(8,128)(2,1)S(1)}, u32[]{:S(2)}, u32[]{:S(2)}) collective-permute-start(bf16[6400,128]{1,0:T(8,128)(2,1)S(1)} %get-tuple-element.225.refs_3_), channel_id=1, source_target_pairs={{2,0},{3,1},{4,2},{5,3},{6,4},{7,5},{0,6},{1,7},{10,8},{11,9},{12,... | collective-permute-start | bytes 4915208 | tf_op jit(solution)/shard_map/ppermute | solution.py:534
  220.9 22.2 %collective-permute-start.23 = (f32[1600,128]{1,0:T(8,128)S(1)}, f32[1600,128]{1,0:T(8,128)S(1)}, u32[]{:S(2)}, u32[]{:S(2)}) collective-permute-start(f32[1600,128]{1,0:T(8,128)S(1)} %get-tuple-element.223.refs_3_), channel_id=1, source_target_pairs={{0,2},{1,3},{2,4},{3,5},{4,6},{5,7},{6,0},{7,1},{8,10},{9,11},{10,... | collective-permute-start | bytes 2457608 | tf_op jit(solution)/shard_map/ppermute | solution.py:540
  222.9 37.7 %collective-permute-start.22 = (f32[1600,128]{1,0:T(8,128)S(1)}, f32[1600,128]{1,0:T(8,128)S(1)}, u32[]{:S(2)}, u32[]{:S(2)}) collective-permute-start(f32[1600,128]{1,0:T(8,128)S(1)} %get-tuple-element.224.refs_4_), channel_id=1, source_target_pairs={{0,2},{1,3},{2,4},{3,5},{4,6},{5,7},{6,0},{7,1},{8,10},{9,11},{10,... | collective-permute-start | bytes 2457608 | tf_op jit(solution)/shard_map/ppermute | solution.py:540
  224.2 43.4 %collective-permute-start.19 = (f32[552,128]{1,0:T(8,128)S(1)}, f32[552,128]{1,0:T(8,128)S(1)}, u32[]{:S(2)}, u32[]{:S(2)}) collective-permute-start(f32[552,128]{1,0:T(8,128)S(1)} %get-tuple-element.231), channel_id=1, source_target_pairs={{0,2},{1,3},{2,0},{3,1},{4,6},{5,7},{6,4},{7,5},{8,10},{9,11},{10,... | collective-permute-start | bytes 847880 | tf_op jit(solution)/shard_map/ppermute | solution.py:554
  225.8 41.8 %collective-permute-start.20 = (f32[552,128]{1,0:T(8,128)S(1)}, f32[552,128]{1,0:T(8,128)S(1)}, u32[]{:S(2)}, u32[]{:S(2)}) collective-permute-start(f32[552,128]{1,0:T(8,128)S(1)} %get-tuple-element.232), channel_id=1, source_target_pairs={{0,4},{1,5},{2,6},{3,7},{4,0},{5,1},{6,2},{7,3},{8,12},{9,13},{10,... | collective-permute-start | bytes 847880 | tf_op jit(solution)/shard_map/ppermute | solution.py:554
  226.8 45.4 %collective-permute-start.21 = (f32[552,128]{1,0:T(8,128)S(1)}, f32[552,128]{1,0:T(8,128)S(1)}, u32[]{:S(2)}, u32[]{:S(2)}) collective-permute-start(f32[552,128]{1,0:T(8,128)S(1)} %get-tuple-element.233), channel_id=1, source_target_pairs={{0,6},{1,7},{2,4},{3,5},{4,2},{5,3},{6,0},{7,1},{8,14},{9,15},{10,... | collective-permute-start | bytes 847880 | tf_op jit(solution)/shard_map/ppermute | solution.py:554
  272.3 24.8 %collective-permute-start.24 = (f32[552,128]{1,0:T(8,128)S(1)}, f32[552,128]{1,0:T(8,128)S(1)}, u32[]{:S(2)}, u32[]{:S(2)}) collective-permute-start(f32[552,128]{1,0:T(8,128)S(1)} %get-tuple-element.237.refs_0_), channel_id=1, source_target_pairs={{0,2},{1,3},{2,0},{3,1},{4,6},{5,7},{6,4},{7,5},{8,10},{9,11},{10,... | collective-permute-start | bytes 847880 | tf_op jit(solution)/shard_map/ppermute | solution.py:558
  273.7 23.4 %collective-permute-start.25 = (f32[552,128]{1,0:T(8,128)S(1)}, f32[552,128]{1,0:T(8,128)S(1)}, u32[]{:S(2)}, u32[]{:S(2)}) collective-permute-start(f32[552,128]{1,0:T(8,128)S(1)} %get-tuple-element.237.refs_0_), channel_id=1, source_target_pairs={{0,4},{1,5},{2,6},{3,7},{4,0},{5,1},{6,2},{7,3},{8,12},{9,13},{10,... | collective-permute-start | bytes 847880 | tf_op jit(solution)/shard_map/ppermute | solution.py:558
  274.7 22.4 %collective-permute-start.26 = (f32[552,128]{1,0:T(8,128)S(1)}, f32[552,128]{1,0:T(8,128)S(1)}, u32[]{:S(2)}, u32[]{:S(2)}) collective-permute-start(f32[552,128]{1,0:T(8,128)S(1)} %get-tuple-element.237.refs_0_), channel_id=1, source_target_pairs={{0,6},{1,7},{2,4},{3,5},{4,2},{5,3},{6,0},{7,1},{8,14},{9,15},{10,... | collective-permute-start | bytes 847880 | tf_op jit(solution)/shard_map/ppermute | solution.py:558
  341.1 33.8 %collective-permute-start.34 = (f32[1600,128]{1,0:T(8,128)S(1)}, f32[1600,128]{1,0:T(8,128)S(1)}, u32[]{:S(2)}, u32[]{:S(2)}) collective-permute-start(f32[1600,128]{1,0:T(8,128)S(1)} %get-tuple-element.246.refs_3_), channel_id=1, source_target_pairs={{0,3},{1,4},{2,5},{3,6},{4,7},{5,0},{6,1},{7,2},{8,11},{9,12},{10,... | collective-permute-start | bytes 2457608 | tf_op jit(solution)/shard_map/ppermute | solution.py:540
  359.0 37.7 %collective-permute-start.33 = (f32[1600,128]{1,0:T(8,128)S(1)}, f32[1600,128]{1,0:T(8,128)S(1)}, u32[]{:S(2)}, u32[]{:S(2)}) collective-permute-start(f32[1600,128]{1,0:T(8,128)S(1)} %get-tuple-element.247.refs_4_), channel_id=1, source_target_pairs={{0,3},{1,4},{2,5},{3,6},{4,7},{5,0},{6,1},{7,2},{8,11},{9,12},{10,... | collective-permute-start | bytes 2457608 | tf_op jit(solution)/shard_map/ppermute | solution.py:540
  360.2 43.4 %collective-permute-start.30 = (f32[552,128]{1,0:T(8,128)S(1)}, f32[552,128]{1,0:T(8,128)S(1)}, u32[]{:S(2)}, u32[]{:S(2)}) collective-permute-start(f32[552,128]{1,0:T(8,128)S(1)} %get-tuple-element.254), channel_id=1, source_target_pairs={{0,2},{1,3},{2,0},{3,1},{4,6},{5,7},{6,4},{7,5},{8,10},{9,11},{10,... | collective-permute-start | bytes 847880 | tf_op jit(solution)/shard_map/ppermute | solution.py:554
  361.9 41.7 %collective-permute-start.31 = (f32[552,128]{1,0:T(8,128)S(1)}, f32[552,128]{1,0:T(8,128)S(1)}, u32[]{:S(2)}, u32[]{:S(2)}) collective-permute-start(f32[552,128]{1,0:T(8,128)S(1)} %get-tuple-element.255), channel_id=1, source_target_pairs={{0,4},{1,5},{2,6},{3,7},{4,0},{5,1},{6,2},{7,3},{8,12},{9,13},{10,... | collective-permute-start | bytes 847880 | tf_op jit(solution)/shard_map/ppermute | solution.py:554
  362.9 40.7 %collective-permute-start.32 = (f32[552,128]{1,0:T(8,128)S(1)}, f32[552,128]{1,0:T(8,128)S(1)}, u32[]{:S(2)}, u32[]{:S(2)}) collective-permute-start(f32[552,128]{1,0:T(8,128)S(1)} %get-tuple-element.256), channel_id=1, source_target_pairs={{0,6},{1,7},{2,4},{3,5},{4,2},{5,3},{6,0},{7,1},{8,14},{9,15},{10,... | collective-permute-start | bytes 847880 | tf_op jit(solution)/shard_map/ppermute | solution.py:554
  403.7 24.8 %collective-permute-start.35 = (f32[552,128]{1,0:T(8,128)S(1)}, f32[552,128]{1,0:T(8,128)S(1)}, u32[]{:S(2)}, u32[]{:S(2)}) collective-permute-start(f32[552,128]{1,0:T(8,128)S(1)} %get-tuple-element.260.refs_0_), channel_id=1, source_target_pairs={{0,2},{1,3},{2,0},{3,1},{4,6},{5,7},{6,4},{7,5},{8,10},{9,11},{10,... | collective-permute-start | bytes 847880 | tf_op jit(solution)/shard_map/ppermute | solution.py:558
  403.7 24.8 %collective-permute-start.36 = (f32[552,128]{1,0:T(8,128)S(1)}, f32[552,128]{1,0:T(8,128)S(1)}, u32[]{:S(2)}, u32[]{:S(2)}) collective-permute-start(f32[552,128]{1,0:T(8,128)S(1)} %get-tuple-element.260.refs_0_), channel_id=1, source_target_pairs={{0,4},{1,5},{2,6},{3,7},{4,0},{5,1},{6,2},{7,3},{8,12},{9,13},{10,... | collective-permute-start | bytes 847880 | tf_op jit(solution)/shard_map/ppermute | solution.py:558
  404.8 23.7 %collective-permute-start.37 = (f32[552,128]{1,0:T(8,128)S(1)}, f32[552,128]{1,0:T(8,128)S(1)}, u32[]{:S(2)}, u32[]{:S(2)}) collective-permute-start(f32[552,128]{1,0:T(8,128)S(1)} %get-tuple-element.260.refs_0_), channel_id=1, source_target_pairs={{0,6},{1,7},{2,4},{3,5},{4,2},{5,3},{6,0},{7,1},{8,14},{9,15},{10,... | collective-permute-start | bytes 847880 | tf_op jit(solution)/shard_map/ppermute | solution.py:558
  432.5 35.6 %collective-permute-start.38 = (bf16[6400,128]{1,0:T(8,128)(2,1)S(1)}, bf16[6400,128]{1,0:T(8,128)(2,1)S(1)}, u32[]{:S(2)}, u32[]{:S(2)}) collective-permute-start(bf16[6400,128]{1,0:T(8,128)(2,1)S(1)} %get-tuple-element.267.refs_3_), channel_id=1, source_target_pairs={{4,0},{5,1},{6,2},{7,3},{0,4},{1,5},{2,6},{3,7},{12,8},{13,9},{14,... | collective-permute-start | bytes 4915208 | tf_op jit(solution)/shard_map/ppermute | solution.py:534
  487.8 27.2 %collective-permute-start.45 = (f32[1600,128]{1,0:T(8,128)S(1)}, f32[1600,128]{1,0:T(8,128)S(1)}, u32[]{:S(2)}, u32[]{:S(2)}) collective-permute-start(f32[1600,128]{1,0:T(8,128)S(1)} %get-tuple-element.265.refs_3_), channel_id=1, source_target_pairs={{0,4},{1,5},{2,6},{3,7},{4,0},{5,1},{6,2},{7,3},{8,12},{9,13},{10,... | collective-permute-start | bytes 2457608 | tf_op jit(solution)/shard_map/ppermute | solution.py:540
  488.8 43.7 %collective-permute-start.44 = (f32[1600,128]{1,0:T(8,128)S(1)}, f32[1600,128]{1,0:T(8,128)S(1)}, u32[]{:S(2)}, u32[]{:S(2)}) collective-permute-start(f32[1600,128]{1,0:T(8,128)S(1)} %get-tuple-element.266.refs_4_), channel_id=1, source_target_pairs={{0,4},{1,5},{2,6},{3,7},{4,0},{5,1},{6,2},{7,3},{8,12},{9,13},{10,... | collective-permute-start | bytes 2457608 | tf_op jit(solution)/shard_map/ppermute | solution.py:540
  490.7 48.7 %collective-permute-start.41 = (f32[552,128]{1,0:T(8,128)S(1)}, f32[552,128]{1,0:T(8,128)S(1)}, u32[]{:S(2)}, u32[]{:S(2)}) collective-permute-start(f32[552,128]{1,0:T(8,128)S(1)} %get-tuple-element.273), channel_id=1, source_target_pairs={{0,2},{1,3},{2,0},{3,1},{4,6},{5,7},{6,4},{7,5},{8,10},{9,11},{10,... | collective-permute-start | bytes 847880 | tf_op jit(solution)/shard_map/ppermute | solution.py:554
  491.1 48.4 %collective-permute-start.42 = (f32[552,128]{1,0:T(8,128)S(1)}, f32[552,128]{1,0:T(8,128)S(1)}, u32[]{:S(2)}, u32[]{:S(2)}) collective-permute-start(f32[552,128]{1,0:T(8,128)S(1)} %get-tuple-element.274), channel_id=1, source_target_pairs={{0,4},{1,5},{2,6},{3,7},{4,0},{5,1},{6,2},{7,3},{8,12},{9,13},{10,... | collective-permute-start | bytes 847880 | tf_op jit(solution)/shard_map/ppermute | solution.py:554
  492.1 47.4 %collective-permute-start.43 = (f32[552,128]{1,0:T(8,128)S(1)}, f32[552,128]{1,0:T(8,128)S(1)}, u32[]{:S(2)}, u32[]{:S(2)}) collective-permute-start(f32[552,128]{1,0:T(8,128)S(1)} %get-tuple-element.275), channel_id=1, source_target_pairs={{0,6},{1,7},{2,4},{3,5},{4,2},{5,3},{6,0},{7,1},{8,14},{9,15},{10,... | collective-permute-start | bytes 847880 | tf_op jit(solution)/shard_map/ppermute | solution.py:554
  539.5 24.8 %collective-permute-start.46 = (f32[552,128]{1,0:T(8,128)S(1)}, f32[552,128]{1,0:T(8,128)S(1)}, u32[]{:S(2)}, u32[]{:S(2)}) collective-permute-start(f32[552,128]{1,0:T(8,128)S(1)} %get-tuple-element.279.refs_0_), channel_id=1, source_target_pairs={{0,2},{1,3},{2,0},{3,1},{4,6},{5,7},{6,4},{7,5},{8,10},{9,11},{10,... | collective-permute-start | bytes 847880 | tf_op jit(solution)/shard_map/ppermute | solution.py:558
  539.9 24.5 %collective-permute-start.47 = (f32[552,128]{1,0:T(8,128)S(1)}, f32[552,128]{1,0:T(8,128)S(1)}, u32[]{:S(2)}, u32[]{:S(2)}) collective-permute-start(f32[552,128]{1,0:T(8,128)S(1)} %get-tuple-element.279.refs_0_), channel_id=1, source_target_pairs={{0,4},{1,5},{2,6},{3,7},{4,0},{5,1},{6,2},{7,3},{8,12},{9,13},{10,... | collective-permute-start | bytes 847880 | tf_op jit(solution)/shard_map/ppermute | solution.py:558
  540.9 23.5 %collective-permute-start.48 = (f32[552,128]{1,0:T(8,128)S(1)}, f32[552,128]{1,0:T(8,128)S(1)}, u32[]{:S(2)}, u32[]{:S(2)}) collective-permute-start(f32[552,128]{1,0:T(8,128)S(1)} %get-tuple-element.279.refs_0_), channel_id=1, source_target_pairs={{0,6},{1,7},{2,4},{3,5},{4,2},{5,3},{6,0},{7,1},{8,14},{9,15},{10,... | collective-permute-start | bytes 847880 | tf_op jit(solution)/shard_map/ppermute | solution.py:558
  568.4 37.5 %collective-permute-start.49 = (bf16[6400,128]{1,0:T(8,128)(2,1)S(1)}, bf16[6400,128]{1,0:T(8,128)(2,1)S(1)}, u32[]{:S(2)}, u32[]{:S(2)}) collective-permute-start(bf16[6400,128]{1,0:T(8,128)(2,1)S(1)} %get-tuple-element.283.refs_3_), channel_id=1, source_target_pairs={{5,0},{6,1},{7,2},{0,3},{1,4},{2,5},{3,6},{4,7},{13,8},{14,9},{15,... | collective-permute-start | bytes 4915208 | tf_op jit(solution)/shard_map/ppermute | solution.py:534
  626.4 25.5 %collective-permute-start.55 = (f32[1600,128]{1,0:T(8,128)S(1)}, f32[1600,128]{1,0:T(8,128)S(1)}, u32[]{:S(2)}, u32[]{:S(2)}) collective-permute-start(f32[1600,128]{1,0:T(8,128)S(1)} %get-tuple-element.289.refs_4_), channel_id=1, source_target_pairs={{0,5},{1,6},{2,7},{3,0},{4,1},{5,2},{6,3},{7,4},{8,13},{9,14},{10,... | collective-permute-start | bytes 2457608 | tf_op jit(solution)/shard_map/ppermute | solution.py:540
  628.2 30.6 %collective-permute-start.52 = (f32[552,128]{1,0:T(8,128)S(1)}, f32[552,128]{1,0:T(8,128)S(1)}, u32[]{:S(2)}, u32[]{:S(2)}) collective-permute-start(f32[552,128]{1,0:T(8,128)S(1)} %get-tuple-element.296), channel_id=1, source_target_pairs={{0,2},{1,3},{2,0},{3,1},{4,6},{5,7},{6,4},{7,5},{8,10},{9,11},{10,... | collective-permute-start | bytes 847880 | tf_op jit(solution)/shard_map/ppermute | solution.py:554
  628.3 30.5 %collective-permute-start.53 = (f32[552,128]{1,0:T(8,128)S(1)}, f32[552,128]{1,0:T(8,128)S(1)}, u32[]{:S(2)}, u32[]{:S(2)}) collective-permute-start(f32[552,128]{1,0:T(8,128)S(1)} %get-tuple-element.297), channel_id=1, source_target_pairs={{0,4},{1,5},{2,6},{3,7},{4,0},{5,1},{6,2},{7,3},{8,12},{9,13},{10,... | collective-permute-start | bytes 847880 | tf_op jit(solution)/shard_map/ppermute | solution.py:554
  629.3 29.5 %collective-permute-start.54 = (f32[552,128]{1,0:T(8,128)S(1)}, f32[552,128]{1,0:T(8,128)S(1)}, u32[]{:S(2)}, u32[]{:S(2)}) collective-permute-start(f32[552,128]{1,0:T(8,128)S(1)} %get-tuple-element.298), channel_id=1, source_target_pairs={{0,6},{1,7},{2,4},{3,5},{4,2},{5,3},{6,0},{7,1},{8,14},{9,15},{10,... | collective-permute-start | bytes 847880 | tf_op jit(solution)/shard_map/ppermute | solution.py:554
  658.9 34.0 %collective-permute-start.57 = (f32[552,128]{1,0:T(8,128)S(1)}, f32[552,128]{1,0:T(8,128)S(1)}, u32[]{:S(2)}, u32[]{:S(2)}) collective-permute-start(f32[552,128]{1,0:T(8,128)S(1)} %get-tuple-element.302.refs_0_), channel_id=1, source_target_pairs={{0,2},{1,3},{2,0},{3,1},{4,6},{5,7},{6,4},{7,5},{8,10},{9,11},{10,... | collective-permute-start | bytes 847880 | tf_op jit(solution)/shard_map/ppermute | solution.py:558
  670.1 22.8 %collective-permute-start.58 = (f32[552,128]{1,0:T(8,128)S(1)}, f32[552,128]{1,0:T(8,128)S(1)}, u32[]{:S(2)}, u32[]{:S(2)}) collective-permute-start(f32[552,128]{1,0:T(8,128)S(1)} %get-tuple-element.302.refs_0_), channel_id=1, source_target_pairs={{0,4},{1,5},{2,6},{3,7},{4,0},{5,1},{6,2},{7,3},{8,12},{9,13},{10,... | collective-permute-start | bytes 847880 | tf_op jit(solution)/shard_map/ppermute | solution.py:558
  696.9 39.4 %collective-permute-start.60 = (bf16[6400,128]{1,0:T(8,128)(2,1)S(1)}, bf16[6400,128]{1,0:T(8,128)(2,1)S(1)}, u32[]{:S(2)}, u32[]{:S(2)}) collective-permute-start(bf16[6400,128]{1,0:T(8,128)(2,1)S(1)} %get-tuple-element.309.refs_3_), channel_id=1, source_target_pairs={{6,0},{7,1},{0,2},{1,3},{2,4},{3,5},{4,6},{5,7},{14,8},{15,9},{8,1... | collective-permute-start | bytes 4915208 | tf_op jit(solution)/shard_map/ppermute | solution.py:534
  757.0 37.4 %collective-permute-start.66 = (f32[1600,128]{1,0:T(8,128)S(1)}, f32[1600,128]{1,0:T(8,128)S(1)}, u32[]{:S(2)}, u32[]{:S(2)}) collective-permute-start(f32[1600,128]{1,0:T(8,128)S(1)} %get-tuple-element.308.refs_4_), channel_id=1, source_target_pairs={{0,6},{1,7},{2,0},{3,1},{4,2},{5,3},{6,4},{7,5},{8,14},{9,15},{10,... | collective-permute-start | bytes 2457608 | tf_op jit(solution)/shard_map/ppermute | solution.py:540
  758.7 42.7 %collective-permute-start.63 = (f32[552,128]{1,0:T(8,128)S(1)}, f32[552,128]{1,0:T(8,128)S(1)}, u32[]{:S(2)}, u32[]{:S(2)}) collective-permute-start(f32[552,128]{1,0:T(8,128)S(1)} %get-tuple-element.315), channel_id=1, source_target_pairs={{0,2},{1,3},{2,0},{3,1},{4,6},{5,7},{6,4},{7,5},{8,10},{9,11},{10,... | collective-permute-start | bytes 847880 | tf_op jit(solution)/shard_map/ppermute | solution.py:554
  759.5 41.8 %collective-permute-start.64 = (f32[552,128]{1,0:T(8,128)S(1)}, f32[552,128]{1,0:T(8,128)S(1)}, u32[]{:S(2)}, u32[]{:S(2)}) collective-permute-start(f32[552,128]{1,0:T(8,128)S(1)} %get-tuple-element.316), channel_id=1, source_target_pairs={{0,4},{1,5},{2,6},{3,7},{4,0},{5,1},{6,2},{7,3},{8,12},{9,13},{10,... | collective-permute-start | bytes 847880 | tf_op jit(solution)/shard_map/ppermute | solution.py:554
  760.5 46.0 %collective-permute-start.65 = (f32[552,128]{1,0:T(8,128)S(1)}, f32[552,128]{1,0:T(8,128)S(1)}, u32[]{:S(2)}, u32[]{:S(2)}) collective-permute-start(f32[552,128]{1,0:T(8,128)S(1)} %get-tuple-element.317), channel_id=1, source_target_pairs={{0,6},{1,7},{2,4},{3,5},{4,2},{5,3},{6,0},{7,1},{8,14},{9,15},{10,... | collective-permute-start | bytes 847880 | tf_op jit(solution)/shard_map/ppermute | solution.py:554
  806.6 25.1 %collective-permute-start.68 = (f32[552,128]{1,0:T(8,128)S(1)}, f32[552,128]{1,0:T(8,128)S(1)}, u32[]{:S(2)}, u32[]{:S(2)}) collective-permute-start(f32[552,128]{1,0:T(8,128)S(1)} %get-tuple-element.321.refs_0_), channel_id=1, source_target_pairs={{0,2},{1,3},{2,0},{3,1},{4,6},{5,7},{6,4},{7,5},{8,10},{9,11},{10,... | collective-permute-start | bytes 847880 | tf_op jit(solution)/shard_map/ppermute | solution.py:558
  807.9 23.8 %collective-permute-start.69 = (f32[552,128]{1,0:T(8,128)S(1)}, f32[552,128]{1,0:T(8,128)S(1)}, u32[]{:S(2)}, u32[]{:S(2)}) collective-permute-start(f32[552,128]{1,0:T(8,128)S(1)} %get-tuple-element.321.refs_0_), channel_id=1, source_target_pairs={{0,4},{1,5},{2,6},{3,7},{4,0},{5,1},{6,2},{7,3},{8,12},{9,13},{10,... | collective-permute-start | bytes 847880 | tf_op jit(solution)/shard_map/ppermute | solution.py:558
  808.9 22.8 %collective-permute-start.70 = (f32[552,128]{1,0:T(8,128)S(1)}, f32[552,128]{1,0:T(8,128)S(1)}, u32[]{:S(2)}, u32[]{:S(2)}) collective-permute-start(f32[552,128]{1,0:T(8,128)S(1)} %get-tuple-element.321.refs_0_), channel_id=1, source_target_pairs={{0,6},{1,7},{2,4},{3,5},{4,2},{5,3},{6,0},{7,1},{8,14},{9,15},{10,... | collective-permute-start | bytes 847880 | tf_op jit(solution)/shard_map/ppermute | solution.py:558
  (34 other events, 356.3 us)
Sparse Core Ops, SparseCore 0:
  16.1 5.0 sort.23.cloned.1.call-done
  24.5 11.4 sort.21.cloned.1.call-done
  (2 shorter events, 0.0 us)
where the time goes:
time: 876 us; the launch traced here: 865 us
  Pallas kernels  412 us (47%)
  waiting for transfers between devices  310 us (35%)
  starting transfers between devices  101 us (12%)
  local copies, waits for them, and re-layouts  23.9 us (3%)
  between operations  15.4 us (2%)
    pallas_call x61, Pallas kernels, call(): pl.pallas_call(body, in_specs=in_specs + [VM], out_specs=[VM] + out_specs...  376 us
    ppermute x6, waiting for transfers between devices, train(): far_tails = lax.ppermute(tails, 'ent', to_asker)  156 us
    ppermute x12, waiting for transfers between devices, train(): far_heads.append(lax.ppermute(heads[side], 'ent', to_owner))  134 us
    ppermute x18, starting transfers between devices, train(): totals = [lax.ppermute(total, 'ent', away(2 * hop + 2)) for hop in range(3)]  30.3 us
    ppermute x12, starting transfers between devices, train(): far_heads.append(lax.ppermute(heads[side], 'ent', to_owner))  29.6 us
    ppermute x18, starting transfers between devices, train(): lax.ppermute(x, 'ent', away(2 * hop + 2))  21.1 us
    pallas_call x1, Pallas kernels, train(): pl.pallas_call(store_kernel, grid=(part_rows // cols,), in_specs=[VM], ou...  19.5 us
  transfers between devices with their start and end apart: 72, of which 31 were waited for; matrix products, arithmetic and copies ran while one was open for 1% of the time, Pallas kernels for 27%

commit v1 on v0

--- a/solution.py
+++ b/solution.py
@@ -27,7 +27,7 @@
 
 
 def params(mib):
-    return pltpu.CompilerParams(vmem_limit_bytes=mib * MIB)
+    return pltpu.CompilerParams(vmem_limit_bytes=int(mib * MIB))
 
 
 def lane_ids(shape):
@@ -74,12 +74,22 @@
     ref2[pl.ds(start * 4 + part, rows, stride=4), :] = x
 
 
-def copy_rows(idx_ref, count, src, dst, offset):
-    def body(i, carry):
-        dst[offset + i] = src[idx_ref[i]]
+def each(count, body, carry=0, base=0, unroll=16):
+    def step(b, carry):
+        at = b * unroll
+        for u in range(unroll):
+            carry = body(base + at, at, u, carry)
         return carry
 
-    lax.fori_loop(0, count, body, 0, unroll=16)
+    return lax.fori_loop(0, count // unroll, step, carry)
+
+
+def copy_rows(idx_ref, count, src, dst, skip=0):
+    def body(base, at, u, carry):
+        dst[at + u] = src[idx_ref[base + (skip + u)]]
+        return carry
+
+    each(count, body)
 
 
 def pack_rows(dst, src2, rows, first, groups, packed):
@@ -201,15 +211,15 @@
 def gather_tails_kernel(tail_ref, neg_ref, tail_out, tab_ref, hold_ref, *, areas):
     edges = tail_ref.shape[0]
     hold2 = flat(hold_ref)
-    copy_rows(tail_ref, edges, tab_ref, hold_ref, 0)
+    copy_rows(tail_ref, edges, tab_ref, hold_ref)
     packed = pack_rows(tail_out, hold2, 2 * edges, 0, 4, None)
-    copy_rows(neg_ref, edges, tab_ref, hold_ref, 0)
+    copy_rows(neg_ref, edges, tab_ref, hold_ref)
     pack_rows(tail_out, hold2, 2 * edges, 4, 4, packed)
 
 
 def gather_heads_kernel(head_ref, one_out, two_out, tab_ref, hold_ref, *, areas):
     edges = head_ref.shape[0]
-    copy_rows(head_ref, edges, tab_ref, hold_ref, 0)
+    copy_rows(head_ref, edges, tab_ref, hold_ref)
     for side, out in enumerate((one_out, two_out)):
         half = hold_ref.at[pl.ds(side * (edges // 2), edges // 2)]
         pack_rows(out, flat(half), edges // 2, 0, 8, None)
@@ -226,27 +236,22 @@
     return new
 
 
-def apply_rows(key_ref, grad_ref, tab_ref, sum_ref, row_ref):
+def apply_rows(plan_ref, same_ref, grad_ref, tab_ref, sum_ref, row_ref):
     size = sum_ref.shape[0]
+    count = same_ref.shape[0]
     sum2, row2 = flat(sum_ref), flat(row_ref)
     block = 128
 
-    def chunk(c, carry):
+    def chunk(c, acc):
         base = c * size
 
-        def collect(e, carry):
-            prev, acc, old = carry
-            key = key_ref[base + e]
-            row = key >> 12
-            same = row == prev
-            g = grad_ref[key & 4095]
-            acc = jnp.where(same, acc + g, g)
-            old = jnp.where(same, old, tab_ref[row])
-            sum_ref[e] = acc
-            row_ref[e] = old
-            return row, acc, old
-
-        carry = lax.fori_loop(0, size, collect, carry, unroll=16)
+        def collect(base, at, u, acc):
+            acc = acc * same_ref[base + u] + grad_ref[plan_ref[base + u]]
+            sum_ref[at + u] = acc
+            row_ref[at + u] = tab_ref[plan_ref[base + (count + u)]]
+            return acc
+
+        acc = each(size, collect, acc, base)
 
         def update(b, carry):
             at = b * (block * 4)
@@ -259,19 +264,18 @@
 
         lax.fori_loop(0, size // block, update, 0)
 
-        def write(e, carry):
-            tab_ref[key_ref[base + e] >> 12] = row_ref[e]
+        def write(base, at, u, carry):
+            tab_ref[plan_ref[base + (2 * count + u)]] = row_ref[at + u]
             return carry
 
-        lax.fori_loop(0, size, write, 0, unroll=16)
-        return carry
-
-    zero = jnp.zeros((4, LANES), F32)
-    lax.fori_loop(0, key_ref.shape[0] // size, chunk, (jnp.int32(-1), zero, zero))
-
-
-def update_kernel(key_ref, tab_ref, sum_ref, row_ref, *, areas):
-    apply_rows(key_ref, tab_ref.at[pl.ds(*areas['grad'])], tab_ref, sum_ref, row_ref)
+        each(size, write, 0, base)
+        return acc
+
+    lax.fori_loop(0, count // size, chunk, jnp.zeros((4, LANES), F32))
+
+
+def update_kernel(plan_ref, same_ref, tab_ref, sum_ref, row_ref, *, areas):
+    apply_rows(plan_ref, same_ref, tab_ref.at[pl.ds(*areas['grad'])], tab_ref, sum_ref, row_ref)
 
 
 def put_wide(ref, start, rows, planes):
@@ -304,11 +308,11 @@
     return planes
 
 
-def head_kernel(rel_ref, key_ref, weight_ref, one_ref, two_ref, tail_ref, give_out, tab_ref, query_ref, neg_ref, *, areas, step_no):
+def head_kernel(rel_ref, plan_ref, same_ref, weight_ref, one_ref, two_ref, tail_ref, give_out, tab_ref, query_ref, neg_ref, *, areas, step_no):
     rel_tab, grad_out = tab_ref.at[pl.ds(*areas['rel'])], tab_ref.at[pl.ds(*areas['grad'])]
     edges = rel_ref.shape[0]
     hold_ref = grad_out.at[pl.ds(edges, edges)]
-    copy_rows(rel_ref, edges, rel_tab, hold_ref, 0)
+    copy_rows(rel_ref, edges, rel_tab, hold_ref)
     unpack_negs(tail_ref, neg_ref)
     scale = DIM ** -0.5
     for side, head_ref in enumerate((one_ref, two_ref)):
@@ -354,16 +358,12 @@
     sum_ref = grad_out.at[pl.ds(2 * edges, rel_rows)]
     sum_ref[...] = jnp.zeros(sum_ref.shape, F32)
 
-    def scatter(e, carry):
-        prev, acc = carry
-        key = key_ref[e]
-        row = key >> 10
-        g = hold_ref[key & 1023]
-        acc = jnp.where(row == prev, acc + g, g)
-        sum_ref[row] = acc
-        return row, acc
-
-    lax.fori_loop(0, edges, scatter, (jnp.int32(-1), jnp.zeros((4, LANES), F32)), unroll=16)
+    def scatter(base, at, u, acc):
+        acc = acc * same_ref[base + u] + hold_ref[plan_ref[base + u]]
+        sum_ref[plan_ref[base + (edges + u)]] = acc
+        return acc
+
+    each(edges, scatter, jnp.zeros((4, LANES), F32))
     drel_out = flat(tab_ref.at[pl.ds(*areas['drel'])])
     pack_rows(drel_out, flat(sum_ref), rel_rows, 0, 8, None)
     used, half = rel_rows * 25 // 8, give_out.shape[0]
@@ -379,11 +379,7 @@
     hold_ref = grad_out.at[pl.ds(edges + side * half, half)]
     unpack_negs(tail_ref, neg_ref)
 
-    def fetch(i, carry):
-        hold_ref[i] = rel_tab[rel_ref[side * half + i]]
-        return carry
-
-    lax.fori_loop(0, half, fetch, 0, unroll=16)
+    copy_rows(rel_ref, half, rel_tab, hold_ref, side * half)
     put_queries(head_ref, flat(hold_ref), query_ref, 0)
     scale = DIM ** -0.5
     block = edges // 4
@@ -476,9 +472,9 @@
         rounds = head_idx.shape[1]
         edges = head_idx.shape[2]
         rel_rows = -(-rel_count // 128) * 128
+        piece = -(-(rel_rows * 25 // 8) // 64) * 8
         head_idx, tail_idx, rel_idx, neg_idx, edge_mask = (x[0] for x in (head_idx, tail_idx, rel_idx, neg_idx, edge_mask))
 
-        piece = -(-(rel_rows * 25 // 8) // 64) * 8
 
         def away(bits):
             return [(sender, sender ^ bits) for sender in range(ent_devs)]
@@ -495,16 +491,29 @@
         rel_keys = lax.sort(rel_idx * 1024 + jnp.arange(edges, dtype=jnp.int32)[None, :], dimension=1, is_stable=False)
         own_weight = jnp.pad(edge_mask.astype(F32), ((0, 8 - rounds), (0, 0))).T
         serve_weight = served[:, 3].astype(F32).reshape(rounds, edges // 256, 256)
+
+        def plan(keys, bits, spare):
+            rows, places = keys >> bits, keys & ((1 << bits) - 1)
+            equal = rows[:, 1:] == rows[:, :-1]
+            no = jnp.zeros((rounds, 1), jnp.bool_)
+            parts = [places, rows]
+            if spare is not None:
+                parts.append(jnp.where(jnp.concatenate([equal, no], axis=1), spare, rows))
+            return jnp.concatenate(parts, axis=1), jnp.concatenate([no, equal], axis=1).astype(F32)
+
+        total_rows = part_rows + 2 * edges + max(edges, rel_rows) + rel_rows + 2 * piece + rounds
+        moves, same = plan(keys, 12, total_rows)
+        rel_moves, rel_same = plan(rel_keys, 10, None)
         small = []
         for step in range(rounds):
-            small.append((head_idx[step], served[step, 0], served[step, 1], served[step, 2], rel_idx[step], keys[step], rel_keys[step], serve_weight[step]))
+            small.append((head_idx[step], served[step, 0], served[step, 1], served[step, 2], rel_idx[step], moves[step], same[step], rel_moves[step], rel_same[step], serve_weight[step]))
         small, own_weight, rel_cols, ent_cols, ada_row = lax.optimization_barrier((small, own_weight, rel_table.T, ent_part.T, ada_part.reshape(1, part_rows)))
 
         cols = 512
         grad_rows = 2 * edges + max(edges, rel_rows)
         areas = {'grad': (part_rows, grad_rows), 'rel': (part_rows + grad_rows, rel_rows), 'drel': (part_rows + grad_rows + rel_rows, 2 * piece)}
         areas['loss'] = (sum(areas['drel']), rounds)
-        tab_shape = pltpu.VMEM((sum(areas['loss']), 4, LANES), F32)
+        tab_shape = pltpu.VMEM((total_rows + 2, 4, LANES), F32)
         head_wire, tail_wire = shape(edges * 25 // 16, LANES), shape(2 * edges * 25 // 8, LANES, dtype=BF16)
         part_wire, half_wire = shape(piece, LANES), shape(4 * piece, LANES)
         hold = pltpu.VMEM((edges, 4, LANES), F32)
@@ -529,7 +538,7 @@
         half = None
         for step in range(rounds):
             to_owner, to_asker = ring(step)
-            head_ids, serve_tails, serve_negs, serve_rel, own_rel, key, rel_key, weight = small[step]
+            head_ids, serve_tails, serve_negs, serve_rel, own_rel, move, equal, rel_move, rel_equal, weight = small[step]
             tab, (tails,) = call(gather_tails_kernel, tab, [serve_tails, serve_negs], [SM] * 2, [tail_wire], [VM], [hold])
             far_tails = lax.ppermute(tails, 'ent', to_asker)
             tab, heads = call(gather_heads_kernel, tab, [head_ids], [SM], [head_wire] * 2, [VM] * 2, [hold])
@@ -547,7 +556,7 @@
                     [pltpu.VMEM((edges // 2, 512), F32), pltpu.VMEM((edges, 512), BF16), pltpu.VMEM((edges, 512), F32)], side=side, last=last)[0]
 
             tab, (give,) = call(
-                head_kernel, tab, [own_rel, rel_key, own_weight, *heads, far_tails], [SM, SM, VM, VM, VM, VM],
+                head_kernel, tab, [own_rel, rel_move, rel_equal, own_weight, *heads, far_tails], [SM] * 3 + [VM] * 4,
                 [half_wire], [VM], work, step_no=step)
             got = lax.ppermute(give, 'ent', away(1))
             tab, (own, *parts) = call(split_kernel, tab, [got], [VM], [part_wire] * 4, [VM] * 4)
@@ -556,7 +565,7 @@
             tab = tail_role(tab, 1, True)
             tab, (total,) = call(sum_kernel, tab, [own, *parts], [VM] * 4, [part_wire], [VM])
             totals = [lax.ppermute(total, 'ent', away(2 * hop + 2)) for hop in range(3)]
-            tab, _ = call(update_kernel, tab, [key], [SM], [], [], [hold, hold])
+            tab, _ = call(update_kernel, tab, [move, equal], [SM] * 2, [], [], [hold, hold])
             tab, (half,) = call(join_kernel, tab, [total, *totals], [VM] * 4, [half_wire], [VM])
             far_half = lax.ppermute(half, 'ent', away(1))
         tab, _ = call(rel_kernel, tab, [half, far_half], [VM] * 2, [], [])

time: 876 us -> 853 us (0.974)
  Pallas kernels: 412 us -> 383 us
    pallas_call x61, Pallas kernels: 376 us -> 347 us  [call(): pl.pallas_call(body, in_specs=in_specs + [VM], out_specs=[VM] + out_specs...]
  transfers between devices with their start and end apart: 72 -> 72, of which waited for: 31 -> 31; matrix products, arithmetic and copies ran while one was open for 1% -> 1% of each run, Pallas kernels for 27% -> 25%
where the time goes in v1:
time: 853 us; the launch traced here: 842 us
  Pallas kernels  383 us (45%)
  waiting for transfers between devices  314 us (37%)
  starting transfers between devices  100 us (12%)
  local copies, waits for them, and re-layouts  21.6 us (3%)
  between operations  15.5 us (2%)
    pallas_call x61, Pallas kernels, call(): pl.pallas_call(body, in_specs=in_specs + [VM], out_specs=[VM] + out_specs...  347 us
    ppermute x6, waiting for transfers between devices, train(): far_tails = lax.ppermute(tails, 'ent', to_asker)  156 us
    ppermute x12, waiting for transfers between devices, train(): far_heads.append(lax.ppermute(heads[side], 'ent', to_owner))  138 us
    ppermute x18, starting transfers between devices, train(): totals = [lax.ppermute(total, 'ent', away(2 * hop + 2)) for hop in range(3)]  30.3 us
    ppermute x12, starting transfers between devices, train(): far_heads.append(lax.ppermute(heads[side], 'ent', to_owner))  29.6 us
    ppermute x18, starting transfers between devices, train(): lax.ppermute(x, 'ent', away(2 * hop + 2))  21.1 us
    pallas_call x1, Pallas kernels, train(): pl.pallas_call(store_kernel, grid=(part_rows // cols,), in_specs=[VM], ou...  19.5 us
  transfers between devices with their start and end apart: 72, of which 31 were waited for; matrix products, arithmetic and copies ran while one was open for 1% of the time, Pallas kernels for 25%

profile of v1, /device:TPU:0, one launch (start us, length us, event | category | flops | bytes accessed | tf_op | source)
XLA Modules:
  0.0 841.8 jit_solution(5841707591214304873)
XLA Ops:
  25.2 11.0 %sort.17.cloned.1.call-done = s32[6,3072]{1,0:T(8,128)} async-done(((s32[6,3072]{1,0:T(8,128)}), s32[6,3072]{1,0:T(8,128)}) %sort.17.cloned.1.call-update) | async-done | bytes 73744 | tf_op jit(solution)/shard_map/sort | solution.py:490
  38.5 14.5 %load.1.refs_2_ = f32[22360,4,128]{2,1,0:T(4,128)S(1)} custom-call(f32[400,16384]{1,0:T(8,128)} %bitcast.164), custom_call_target="tpu_custom_call" | custom-call | tf_op jit(solution)/shard_map/load/pallas_call | solution.py:533
  53.1 5.1 shard_map.111.refs_2_
  67.0 16.4 %collective-permute-done.6.refs_6_ = bf16[6400,128]{1,0:T(8,128)(2,1)S(1)} collective-permute-done((bf16[6400,128]{1,0:T(8,128)(2,1)S(1)}, bf16[6400,128]{1,0:T(8,128)(2,1)S(1)}, u32[]{:S(2)}, u32[]{:S(2)}) %collective-permute-start.6) | collective-permute-done | bytes 1638432 | tf_op jit(solution)/shard_map/ppermute | solution.py:543
  84.6 17.6 %shard_map.114 = (f32[22360,4,128]{2,1,0:T(4,128)S(1)}, f32[2208,128]{1,0:T(8,128)S(1)}) custom-call(s32[1024]{0:T(1024)S(1)} %bitcast.144, s32[2048]{0:T(1024)S(1)} %bitcast.133, f32[1024]{0:T(1024)S(1)} %bitcast.163, f32[1024,8]{1,0:T(8,128)S(1)} %pad_bitcast_fusion.refs_3_, ...), custom_call_target="tpu_custom_call", output_to_operand_aliasing={{0}: (7, {})} | custom-call | tf_op jit(solution)/shard_map/pallas_call | solution.py:528
  108.8 12.3 %collective-permute-done.12.refs_2_ = f32[1600,128]{1,0:T(8,128)S(1)} collective-permute-done((f32[1600,128]{1,0:T(8,128)S(1)}, f32[1600,128]{1,0:T(8,128)S(1)}, u32[]{:S(2)}, u32[]{:S(2)}) %collective-permute-start.12) | collective-permute-done | bytes 819232 | tf_op jit(solution)/shard_map/ppermute | solution.py:549
  121.1 6.6 shard_map.116.refs_4_
  130.3 7.1 shard_map.117.refs_4_
  141.0 17.8 %shard_map.119.refs_4_ = f32[22360,4,128]{2,1,0:T(4,128)S(1)} custom-call(s32[9216]{0:T(1024)S(1)} %bitcast.108, f32[3072]{0:T(1024)S(1)} %bitcast.115, f32[22360,4,128]{2,1,0:T(4,128)S(1)} %get-tuple-element.239.refs_2_), custom_call_target="tpu_custom_call", output_to_operand_aliasing={{}: (2, {})} | custom-call | tf_op jit(solution)/shard_map/pallas_call | solution.py:528
  169.0 29.7 %collective-permute-done.16.refs_6_ = bf16[6400,128]{1,0:T(8,128)(2,1)S(1)} collective-permute-done((bf16[6400,128]{1,0:T(8,128)(2,1)S(1)}, bf16[6400,128]{1,0:T(8,128)(2,1)S(1)}, u32[]{:S(2)}, u32[]{:S(2)}) %collective-permute-start.16) | collective-permute-done | bytes 1638432 | tf_op jit(solution)/shard_map/ppermute | solution.py:543
  199.9 17.5 %shard_map.124 = (f32[22360,4,128]{2,1,0:T(4,128)S(1)}, f32[2208,128]{1,0:T(8,128)S(1)}) custom-call(s32[1024]{0:T(1024)S(1)} %bitcast.142, s32[2048]{0:T(1024)S(1)} %bitcast.132, f32[1024]{0:T(1024)S(1)} %bitcast.162, f32[1024,8]{1,0:T(8,128)S(1)} %pad_bitcast_fusion.refs_3_, ...), custom_call_target="tpu_custom_call", output_to_operand_aliasing={{0}: (7, {})} | custom-call | tf_op jit(solution)/shard_map/pallas_call | solution.py:528
  224.2 15.4 %collective-permute-done.23.refs_2_ = f32[1600,128]{1,0:T(8,128)S(1)} collective-permute-done((f32[1600,128]{1,0:T(8,128)S(1)}, f32[1600,128]{1,0:T(8,128)S(1)}, u32[]{:S(2)}, u32[]{:S(2)}) %collective-permute-start.23) | collective-permute-done | bytes 819232 | tf_op jit(solution)/shard_map/ppermute | solution.py:549
  239.6 6.6 shard_map.126.refs_4_
  246.3 10.9 %collective-permute-done.22.refs_2_ = f32[1600,128]{1,0:T(8,128)S(1)} collective-permute-done((f32[1600,128]{1,0:T(8,128)S(1)}, f32[1600,128]{1,0:T(8,128)S(1)}, u32[]{:S(2)}, u32[]{:S(2)}) %collective-permute-start.22) | collective-permute-done | bytes 819232 | tf_op jit(solution)/shard_map/ppermute | solution.py:549
  257.1 6.9 shard_map.127.refs_4_
  264.1 4.7 collective-permute-done.21.refs_3_
  272.3 17.8 %shard_map.129.refs_4_ = f32[22360,4,128]{2,1,0:T(4,128)S(1)} custom-call(s32[9216]{0:T(1024)S(1)} %bitcast.107, f32[3072]{0:T(1024)S(1)} %bitcast.114, f32[22360,4,128]{2,1,0:T(4,128)S(1)} %get-tuple-element.259.refs_2_), custom_call_target="tpu_custom_call", output_to_operand_aliasing={{}: (2, {})} | custom-call | tf_op jit(solution)/shard_map/pallas_call | solution.py:528
  300.1 14.6 %collective-permute-done.27.refs_6_ = bf16[6400,128]{1,0:T(8,128)(2,1)S(1)} collective-permute-done((bf16[6400,128]{1,0:T(8,128)(2,1)S(1)}, bf16[6400,128]{1,0:T(8,128)(2,1)S(1)}, u32[]{:S(2)}, u32[]{:S(2)}) %collective-permute-start.27) | collective-permute-done | bytes 1638432 | tf_op jit(solution)/shard_map/ppermute | solution.py:543
  315.9 17.5 %shard_map.134 = (f32[22360,4,128]{2,1,0:T(4,128)S(1)}, f32[2208,128]{1,0:T(8,128)S(1)}) custom-call(s32[1024]{0:T(1024)S(1)} %bitcast.140, s32[2048]{0:T(1024)S(1)} %bitcast.131, f32[1024]{0:T(1024)S(1)} %bitcast.161, f32[1024,8]{1,0:T(8,128)S(1)} %pad_bitcast_fusion.refs_3_, ...), custom_call_target="tpu_custom_call", output_to_operand_aliasing={{0}: (7, {})} | custom-call | tf_op jit(solution)/shard_map/pallas_call | solution.py:528
  333.6 17.8 %collective-permute-start.34 = (f32[1600,128]{1,0:T(8,128)S(1)}, f32[1600,128]{1,0:T(8,128)S(1)}, u32[]{:S(2)}, u32[]{:S(2)}) collective-permute-start(f32[1600,128]{1,0:T(8,128)S(1)} %get-tuple-element.266.refs_4_), channel_id=1, source_target_pairs={{0,3},{1,4},{2,5},{3,6},{4,7},{5,0},{6,1},{7,2},{8,11},{9,12},{10,... | collective-permute-start | bytes 2457608 | tf_op jit(solution)/shard_map/ppermute | solution.py:549
  356.2 11.1 %collective-permute-done.34.refs_2_ = f32[1600,128]{1,0:T(8,128)S(1)} collective-permute-done((f32[1600,128]{1,0:T(8,128)S(1)}, f32[1600,128]{1,0:T(8,128)S(1)}, u32[]{:S(2)}, u32[]{:S(2)}) %collective-permute-start.34) | collective-permute-done | bytes 819232 | tf_op jit(solution)/shard_map/ppermute | solution.py:549
  367.3 6.8 shard_map.136.refs_4_
  374.2 15.0 %collective-permute-done.33.refs_2_ = f32[1600,128]{1,0:T(8,128)S(1)} collective-permute-done((f32[1600,128]{1,0:T(8,128)S(1)}, f32[1600,128]{1,0:T(8,128)S(1)}, u32[]{:S(2)}, u32[]{:S(2)}) %collective-permute-start.33) | collective-permute-done | bytes 819232 | tf_op jit(solution)/shard_map/ppermute | solution.py:549
  389.2 6.8 shard_map.137.refs_4_
  399.6 17.8 %shard_map.139.refs_4_ = f32[22360,4,128]{2,1,0:T(4,128)S(1)} custom-call(s32[9216]{0:T(1024)S(1)} %bitcast.106, f32[3072]{0:T(1024)S(1)} %bitcast.113, f32[22360,4,128]{2,1,0:T(4,128)S(1)} %get-tuple-element.283.refs_2_), custom_call_target="tpu_custom_call", output_to_operand_aliasing={{}: (2, {})} | custom-call | tf_op jit(solution)/shard_map/pallas_call | solution.py:528
  426.9 30.1 %collective-permute-done.38.refs_6_ = bf16[6400,128]{1,0:T(8,128)(2,1)S(1)} collective-permute-done((bf16[6400,128]{1,0:T(8,128)(2,1)S(1)}, bf16[6400,128]{1,0:T(8,128)(2,1)S(1)}, u32[]{:S(2)}, u32[]{:S(2)}) %collective-permute-start.38) | collective-permute-done | bytes 1638432 | tf_op jit(solution)/shard_map/ppermute | solution.py:543
  458.1 18.0 %shard_map.144 = (f32[22360,4,128]{2,1,0:T(4,128)S(1)}, f32[2208,128]{1,0:T(8,128)S(1)}) custom-call(s32[1024]{0:T(1024)S(1)} %bitcast.138, s32[2048]{0:T(1024)S(1)} %bitcast.130, f32[1024]{0:T(1024)S(1)} %bitcast.160, f32[1024,8]{1,0:T(8,128)S(1)} %pad_bitcast_fusion.refs_3_, ...), custom_call_target="tpu_custom_call", output_to_operand_aliasing={{0}: (7, {})} | custom-call | tf_op jit(solution)/shard_map/pallas_call | solution.py:528
  482.5 20.8 %collective-permute-done.45.refs_2_ = f32[1600,128]{1,0:T(8,128)S(1)} collective-permute-done((f32[1600,128]{1,0:T(8,128)S(1)}, f32[1600,128]{1,0:T(8,128)S(1)}, u32[]{:S(2)}, u32[]{:S(2)}) %collective-permute-start.45) | collective-permute-done | bytes 819232 | tf_op jit(solution)/shard_map/ppermute | solution.py:549
  503.3 6.6 shard_map.146.refs_4_
  510.0 10.9 %collective-permute-done.44.refs_2_ = f32[1600,128]{1,0:T(8,128)S(1)} collective-permute-done((f32[1600,128]{1,0:T(8,128)S(1)}, f32[1600,128]{1,0:T(8,128)S(1)}, u32[]{:S(2)}, u32[]{:S(2)}) %collective-permute-start.44) | collective-permute-done | bytes 819232 | tf_op jit(solution)/shard_map/ppermute | solution.py:549
  520.9 6.8 shard_map.147.refs_4_
  531.3 17.8 %shard_map.149.refs_4_ = f32[22360,4,128]{2,1,0:T(4,128)S(1)} custom-call(s32[9216]{0:T(1024)S(1)} %bitcast.105, f32[3072]{0:T(1024)S(1)} %bitcast.112, f32[22360,4,128]{2,1,0:T(4,128)S(1)} %get-tuple-element.303.refs_2_), custom_call_target="tpu_custom_call", output_to_operand_aliasing={{}: (2, {})} | custom-call | tf_op jit(solution)/shard_map/pallas_call | solution.py:528
  558.4 32.3 %collective-permute-done.49.refs_6_ = bf16[6400,128]{1,0:T(8,128)(2,1)S(1)} collective-permute-done((bf16[6400,128]{1,0:T(8,128)(2,1)S(1)}, bf16[6400,128]{1,0:T(8,128)(2,1)S(1)}, u32[]{:S(2)}, u32[]{:S(2)}) %collective-permute-start.49) | collective-permute-done | bytes 1638432 | tf_op jit(solution)/shard_map/ppermute | solution.py:543
  591.8 17.7 %shard_map.154 = (f32[22360,4,128]{2,1,0:T(4,128)S(1)}, f32[2208,128]{1,0:T(8,128)S(1)}) custom-call(s32[1024]{0:T(1024)S(1)} %bitcast.136, s32[2048]{0:T(1024)S(1)} %bitcast.129, f32[1024]{0:T(1024)S(1)} %bitcast.159, f32[1024,8]{1,0:T(8,128)S(1)} %pad_bitcast_fusion.refs_3_, ...), custom_call_target="tpu_custom_call", output_to_operand_aliasing={{0}: (7, {})} | custom-call | tf_op jit(solution)/shard_map/pallas_call | solution.py:528
  616.0 10.7 %collective-permute-done.56.refs_2_ = f32[1600,128]{1,0:T(8,128)S(1)} collective-permute-done((f32[1600,128]{1,0:T(8,128)S(1)}, f32[1600,128]{1,0:T(8,128)S(1)}, u32[]{:S(2)}, u32[]{:S(2)}) %collective-permute-start.56) | collective-permute-done | bytes 819232 | tf_op jit(solution)/shard_map/ppermute | solution.py:549
  626.7 6.6 shard_map.156.refs_4_
  636.2 6.8 shard_map.157.refs_4_
  643.1 11.2 %collective-permute-start.57 = (f32[552,128]{1,0:T(8,128)S(1)}, f32[552,128]{1,0:T(8,128)S(1)}, u32[]{:S(2)}, u32[]{:S(2)}) collective-permute-start(f32[552,128]{1,0:T(8,128)S(1)} %get-tuple-element.324.refs_0_), channel_id=1, source_target_pairs={{0,2},{1,3},{2,0},{3,1},{4,6},{5,7},{6,4},{7,5},{8,10},{9,11},{10,... | collective-permute-start | bytes 847880 | tf_op jit(solution)/shard_map/ppermute | solution.py:567
  655.8 17.8 %shard_map.159.refs_4_ = f32[22360,4,128]{2,1,0:T(4,128)S(1)} custom-call(s32[9216]{0:T(1024)S(1)} %bitcast.104, f32[3072]{0:T(1024)S(1)} %bitcast.111, f32[22360,4,128]{2,1,0:T(4,128)S(1)} %get-tuple-element.327.refs_2_), custom_call_target="tpu_custom_call", output_to_operand_aliasing={{}: (2, {})} | custom-call | tf_op jit(solution)/shard_map/pallas_call | solution.py:528
  684.0 33.0 %collective-permute-done.60.refs_6_ = bf16[6400,128]{1,0:T(8,128)(2,1)S(1)} collective-permute-done((bf16[6400,128]{1,0:T(8,128)(2,1)S(1)}, bf16[6400,128]{1,0:T(8,128)(2,1)S(1)}, u32[]{:S(2)}, u32[]{:S(2)}) %collective-permute-start.60) | collective-permute-done | bytes 1638432 | tf_op jit(solution)/shard_map/ppermute | solution.py:543
  718.2 17.7 %shard_map.164 = (f32[22360,4,128]{2,1,0:T(4,128)S(1)}, f32[2208,128]{1,0:T(8,128)S(1)}) custom-call(s32[1024]{0:T(1024)S(1)} %bitcast.134, s32[2048]{0:T(1024)S(1)} %bitcast.128, f32[1024]{0:T(1024)S(1)} %bitcast.158, f32[1024,8]{1,0:T(8,128)S(1)} %pad_bitcast_fusion.refs_3_, ...), custom_call_target="tpu_custom_call", output_to_operand_aliasing={{0}: (7, {})} | custom-call | tf_op jit(solution)/shard_map/pallas_call | solution.py:528
  742.4 14.8 %collective-permute-done.67.refs_2_ = f32[1600,128]{1,0:T(8,128)S(1)} collective-permute-done((f32[1600,128]{1,0:T(8,128)S(1)}, f32[1600,128]{1,0:T(8,128)S(1)}, u32[]{:S(2)}, u32[]{:S(2)}) %collective-permute-start.67) | collective-permute-done | bytes 819232 | tf_op jit(solution)/shard_map/ppermute | solution.py:549
  757.1 6.6 shard_map.166.refs_4_
  763.7 10.9 %collective-permute-done.66.refs_2_ = f32[1600,128]{1,0:T(8,128)S(1)} collective-permute-done((f32[1600,128]{1,0:T(8,128)S(1)}, f32[1600,128]{1,0:T(8,128)S(1)}, u32[]{:S(2)}, u32[]{:S(2)}) %collective-permute-start.66) | collective-permute-done | bytes 819232 | tf_op jit(solution)/shard_map/ppermute | solution.py:549
  774.7 6.8 shard_map.167.refs_4_
  781.5 5.2 collective-permute-done.65.refs_3_
  790.3 18.0 %shard_map.169.refs_4_ = f32[22360,4,128]{2,1,0:T(4,128)S(1)} custom-call(s32[9216]{0:T(1024)S(1)} %bitcast.103, f32[3072]{0:T(1024)S(1)} %bitcast.110, f32[22360,4,128]{2,1,0:T(4,128)S(1)} %get-tuple-element.347.refs_2_), custom_call_target="tpu_custom_call", output_to_operand_aliasing={{}: (2, {})} | custom-call | tf_op jit(solution)/shard_map/pallas_call | solution.py:528
  812.9 19.5 %store.1 = (f32[400,16384]{1,0:T(8,128)}, f32[1,16384]{1,0:T(1,128)}) custom-call(f32[22360,4,128]{2,1,0:T(4,128)S(1)} %shard_map.171.tab_ref), custom_call_target="tpu_custom_call" | custom-call | tf_op jit(solution)/shard_map/store/pallas_call | solution.py:573
  (223 shorter events, 154.5 us)
Async XLA Ops:
  62.1 21.3 %collective-permute-start.6 = (bf16[6400,128]{1,0:T(8,128)(2,1)S(1)}, bf16[6400,128]{1,0:T(8,128)(2,1)S(1)}, u32[]{:S(2)}, u32[]{:S(2)}) collective-permute-start(bf16[6400,128]{1,0:T(8,128)(2,1)S(1)} %get-tuple-element.218.refs_3_), channel_id=1, source_target_pairs={{1,0},{2,1},{3,2},{4,3},{5,4},{6,5},{7,6},{0,7},{9,8},{10,9},{11,1... | collective-permute-start | bytes 4915208 | tf_op jit(solution)/shard_map/ppermute | solution.py:543
  102.8 27.5 %collective-permute-start.11 = (f32[1600,128]{1,0:T(8,128)S(1)}, f32[1600,128]{1,0:T(8,128)S(1)}, u32[]{:S(2)}, u32[]{:S(2)}) collective-permute-start(f32[1600,128]{1,0:T(8,128)S(1)} %get-tuple-element.224.refs_5_), channel_id=1, source_target_pairs={{0,1},{1,2},{2,3},{3,4},{4,5},{5,6},{6,7},{7,0},{8,9},{9,10},{10,1... | collective-permute-start | bytes 2457608 | tf_op jit(solution)/shard_map/ppermute | solution.py:549
  105.2 32.2 %collective-permute-start.10 = (f32[552,128]{1,0:T(8,128)S(1)}, f32[552,128]{1,0:T(8,128)S(1)}, u32[]{:S(2)}, u32[]{:S(2)}) collective-permute-start(f32[552,128]{1,0:T(8,128)S(1)} %get-tuple-element.232), channel_id=1, source_target_pairs={{0,6},{1,7},{2,4},{3,5},{4,2},{5,3},{6,0},{7,1},{8,14},{9,15},{10,... | collective-permute-start | bytes 847880 | tf_op jit(solution)/shard_map/ppermute | solution.py:563
  107.9 29.5 %collective-permute-start.8 = (f32[552,128]{1,0:T(8,128)S(1)}, f32[552,128]{1,0:T(8,128)S(1)}, u32[]{:S(2)}, u32[]{:S(2)}) collective-permute-start(f32[552,128]{1,0:T(8,128)S(1)} %get-tuple-element.230), channel_id=1, source_target_pairs={{0,2},{1,3},{2,0},{3,1},{4,6},{5,7},{6,4},{7,5},{8,10},{9,11},{10,... | collective-permute-start | bytes 847880 | tf_op jit(solution)/shard_map/ppermute | solution.py:563
  108.4 29.0 %collective-permute-start.9 = (f32[552,128]{1,0:T(8,128)S(1)}, f32[552,128]{1,0:T(8,128)S(1)}, u32[]{:S(2)}, u32[]{:S(2)}) collective-permute-start(f32[552,128]{1,0:T(8,128)S(1)} %get-tuple-element.231), channel_id=1, source_target_pairs={{0,4},{1,5},{2,6},{3,7},{4,0},{5,1},{6,2},{7,3},{8,12},{9,13},{10,... | collective-permute-start | bytes 847880 | tf_op jit(solution)/shard_map/ppermute | solution.py:563
  137.5 21.3 %collective-permute-start.13 = (f32[552,128]{1,0:T(8,128)S(1)}, f32[552,128]{1,0:T(8,128)S(1)}, u32[]{:S(2)}, u32[]{:S(2)}) collective-permute-start(f32[552,128]{1,0:T(8,128)S(1)} %get-tuple-element.236.refs_0_), channel_id=1, source_target_pairs={{0,2},{1,3},{2,0},{3,1},{4,6},{5,7},{6,4},{7,5},{8,10},{9,11},{10,... | collective-permute-start | bytes 847880 | tf_op jit(solution)/shard_map/ppermute | solution.py:567
  138.3 20.5 %collective-permute-start.14 = (f32[552,128]{1,0:T(8,128)S(1)}, f32[552,128]{1,0:T(8,128)S(1)}, u32[]{:S(2)}, u32[]{:S(2)}) collective-permute-start(f32[552,128]{1,0:T(8,128)S(1)} %get-tuple-element.236.refs_0_), channel_id=1, source_target_pairs={{0,4},{1,5},{2,6},{3,7},{4,0},{5,1},{6,2},{7,3},{8,12},{9,13},{10,... | collective-permute-start | bytes 847880 | tf_op jit(solution)/shard_map/ppermute | solution.py:567
  162.8 35.9 %collective-permute-start.16 = (bf16[6400,128]{1,0:T(8,128)(2,1)S(1)}, bf16[6400,128]{1,0:T(8,128)(2,1)S(1)}, u32[]{:S(2)}, u32[]{:S(2)}) collective-permute-start(bf16[6400,128]{1,0:T(8,128)(2,1)S(1)} %get-tuple-element.244.refs_3_), channel_id=1, source_target_pairs={{2,0},{3,1},{4,2},{5,3},{6,4},{7,5},{0,6},{1,7},{10,8},{11,9},{12,... | collective-permute-start | bytes 4915208 | tf_op jit(solution)/shard_map/ppermute | solution.py:543
  217.5 22.2 %collective-permute-start.23 = (f32[1600,128]{1,0:T(8,128)S(1)}, f32[1600,128]{1,0:T(8,128)S(1)}, u32[]{:S(2)}, u32[]{:S(2)}) collective-permute-start(f32[1600,128]{1,0:T(8,128)S(1)} %get-tuple-element.242.refs_4_), channel_id=1, source_target_pairs={{0,2},{1,3},{2,4},{3,5},{4,6},{5,7},{6,0},{7,1},{8,10},{9,11},{10,... | collective-permute-start | bytes 2457608 | tf_op jit(solution)/shard_map/ppermute | solution.py:549
  219.3 37.8 %collective-permute-start.22 = (f32[1600,128]{1,0:T(8,128)S(1)}, f32[1600,128]{1,0:T(8,128)S(1)}, u32[]{:S(2)}, u32[]{:S(2)}) collective-permute-start(f32[1600,128]{1,0:T(8,128)S(1)} %get-tuple-element.243.refs_5_), channel_id=1, source_target_pairs={{0,2},{1,3},{2,4},{3,5},{4,6},{5,7},{6,0},{7,1},{8,10},{9,11},{10,... | collective-permute-start | bytes 2457608 | tf_op jit(solution)/shard_map/ppermute | solution.py:549
  220.7 43.3 %collective-permute-start.19 = (f32[552,128]{1,0:T(8,128)S(1)}, f32[552,128]{1,0:T(8,128)S(1)}, u32[]{:S(2)}, u32[]{:S(2)}) collective-permute-start(f32[552,128]{1,0:T(8,128)S(1)} %get-tuple-element.250), channel_id=1, source_target_pairs={{0,2},{1,3},{2,0},{3,1},{4,6},{5,7},{6,4},{7,5},{8,10},{9,11},{10,... | collective-permute-start | bytes 847880 | tf_op jit(solution)/shard_map/ppermute | solution.py:563
  222.2 41.8 %collective-permute-start.20 = (f32[552,128]{1,0:T(8,128)S(1)}, f32[552,128]{1,0:T(8,128)S(1)}, u32[]{:S(2)}, u32[]{:S(2)}) collective-permute-start(f32[552,128]{1,0:T(8,128)S(1)} %get-tuple-element.251), channel_id=1, source_target_pairs={{0,4},{1,5},{2,6},{3,7},{4,0},{5,1},{6,2},{7,3},{8,12},{9,13},{10,... | collective-permute-start | bytes 847880 | tf_op jit(solution)/shard_map/ppermute | solution.py:563
  223.3 45.4 %collective-permute-start.21 = (f32[552,128]{1,0:T(8,128)S(1)}, f32[552,128]{1,0:T(8,128)S(1)}, u32[]{:S(2)}, u32[]{:S(2)}) collective-permute-start(f32[552,128]{1,0:T(8,128)S(1)} %get-tuple-element.252), channel_id=1, source_target_pairs={{0,6},{1,7},{2,4},{3,5},{4,2},{5,3},{6,0},{7,1},{8,14},{9,15},{10,... | collective-permute-start | bytes 847880 | tf_op jit(solution)/shard_map/ppermute | solution.py:563
  268.8 21.3 %collective-permute-start.24 = (f32[552,128]{1,0:T(8,128)S(1)}, f32[552,128]{1,0:T(8,128)S(1)}, u32[]{:S(2)}, u32[]{:S(2)}) collective-permute-start(f32[552,128]{1,0:T(8,128)S(1)} %get-tuple-element.256.refs_0_), channel_id=1, source_target_pairs={{0,2},{1,3},{2,0},{3,1},{4,6},{5,7},{6,4},{7,5},{8,10},{9,11},{10,... | collective-permute-start | bytes 847880 | tf_op jit(solution)/shard_map/ppermute | solution.py:567
  270.2 19.9 %collective-permute-start.25 = (f32[552,128]{1,0:T(8,128)S(1)}, f32[552,128]{1,0:T(8,128)S(1)}, u32[]{:S(2)}, u32[]{:S(2)}) collective-permute-start(f32[552,128]{1,0:T(8,128)S(1)} %get-tuple-element.256.refs_0_), channel_id=1, source_target_pairs={{0,4},{1,5},{2,6},{3,7},{4,0},{5,1},{6,2},{7,3},{8,12},{9,13},{10,... | collective-permute-start | bytes 847880 | tf_op jit(solution)/shard_map/ppermute | solution.py:567
  294.1 20.6 %collective-permute-start.27 = (bf16[6400,128]{1,0:T(8,128)(2,1)S(1)}, bf16[6400,128]{1,0:T(8,128)(2,1)S(1)}, u32[]{:S(2)}, u32[]{:S(2)}) collective-permute-start(bf16[6400,128]{1,0:T(8,128)(2,1)S(1)} %get-tuple-element.261.refs_3_), channel_id=1, source_target_pairs={{3,0},{4,1},{5,2},{6,3},{7,4},{0,5},{1,6},{2,7},{11,8},{12,9},{13,... | collective-permute-start | bytes 4915208 | tf_op jit(solution)/shard_map/ppermute | solution.py:543
  333.6 33.7 %collective-permute-start.34 = (f32[1600,128]{1,0:T(8,128)S(1)}, f32[1600,128]{1,0:T(8,128)S(1)}, u32[]{:S(2)}, u32[]{:S(2)}) collective-permute-start(f32[1600,128]{1,0:T(8,128)S(1)} %get-tuple-element.266.refs_4_), channel_id=1, source_target_pairs={{0,3},{1,4},{2,5},{3,6},{4,7},{5,0},{6,1},{7,2},{8,11},{9,12},{10,... | collective-permute-start | bytes 2457608 | tf_op jit(solution)/shard_map/ppermute | solution.py:549
  351.4 37.8 %collective-permute-start.33 = (f32[1600,128]{1,0:T(8,128)S(1)}, f32[1600,128]{1,0:T(8,128)S(1)}, u32[]{:S(2)}, u32[]{:S(2)}) collective-permute-start(f32[1600,128]{1,0:T(8,128)S(1)} %get-tuple-element.267.refs_5_), channel_id=1, source_target_pairs={{0,3},{1,4},{2,5},{3,6},{4,7},{5,0},{6,1},{7,2},{8,11},{9,12},{10,... | collective-permute-start | bytes 2457608 | tf_op jit(solution)/shard_map/ppermute | solution.py:549
  352.7 43.3 %collective-permute-start.30 = (f32[552,128]{1,0:T(8,128)S(1)}, f32[552,128]{1,0:T(8,128)S(1)}, u32[]{:S(2)}, u32[]{:S(2)}) collective-permute-start(f32[552,128]{1,0:T(8,128)S(1)} %get-tuple-element.274), channel_id=1, source_target_pairs={{0,2},{1,3},{2,0},{3,1},{4,6},{5,7},{6,4},{7,5},{8,10},{9,11},{10,... | collective-permute-start | bytes 847880 | tf_op jit(solution)/shard_map/ppermute | solution.py:563
  354.3 41.7 %collective-permute-start.31 = (f32[552,128]{1,0:T(8,128)S(1)}, f32[552,128]{1,0:T(8,128)S(1)}, u32[]{:S(2)}, u32[]{:S(2)}) collective-permute-start(f32[552,128]{1,0:T(8,128)S(1)} %get-tuple-element.275), channel_id=1, source_target_pairs={{0,4},{1,5},{2,6},{3,7},{4,0},{5,1},{6,2},{7,3},{8,12},{9,13},{10,... | collective-permute-start | bytes 847880 | tf_op jit(solution)/shard_map/ppermute | solution.py:563
  355.4 40.6 %collective-permute-start.32 = (f32[552,128]{1,0:T(8,128)S(1)}, f32[552,128]{1,0:T(8,128)S(1)}, u32[]{:S(2)}, u32[]{:S(2)}) collective-permute-start(f32[552,128]{1,0:T(8,128)S(1)} %get-tuple-element.276), channel_id=1, source_target_pairs={{0,6},{1,7},{2,4},{3,5},{4,2},{5,3},{6,0},{7,1},{8,14},{9,15},{10,... | collective-permute-start | bytes 847880 | tf_op jit(solution)/shard_map/ppermute | solution.py:563
  396.1 21.3 %collective-permute-start.35 = (f32[552,128]{1,0:T(8,128)S(1)}, f32[552,128]{1,0:T(8,128)S(1)}, u32[]{:S(2)}, u32[]{:S(2)}) collective-permute-start(f32[552,128]{1,0:T(8,128)S(1)} %get-tuple-element.280.refs_0_), channel_id=1, source_target_pairs={{0,2},{1,3},{2,0},{3,1},{4,6},{5,7},{6,4},{7,5},{8,10},{9,11},{10,... | collective-permute-start | bytes 847880 | tf_op jit(solution)/shard_map/ppermute | solution.py:567
  396.2 21.2 %collective-permute-start.36 = (f32[552,128]{1,0:T(8,128)S(1)}, f32[552,128]{1,0:T(8,128)S(1)}, u32[]{:S(2)}, u32[]{:S(2)}) collective-permute-start(f32[552,128]{1,0:T(8,128)S(1)} %get-tuple-element.280.refs_0_), channel_id=1, source_target_pairs={{0,4},{1,5},{2,6},{3,7},{4,0},{5,1},{6,2},{7,3},{8,12},{9,13},{10,... | collective-permute-start | bytes 847880 | tf_op jit(solution)/shard_map/ppermute | solution.py:567
  397.2 20.3 %collective-permute-start.37 = (f32[552,128]{1,0:T(8,128)S(1)}, f32[552,128]{1,0:T(8,128)S(1)}, u32[]{:S(2)}, u32[]{:S(2)}) collective-permute-start(f32[552,128]{1,0:T(8,128)S(1)} %get-tuple-element.280.refs_0_), channel_id=1, source_target_pairs={{0,6},{1,7},{2,4},{3,5},{4,2},{5,3},{6,0},{7,1},{8,14},{9,15},{10,... | collective-permute-start | bytes 847880 | tf_op jit(solution)/shard_map/ppermute | solution.py:567
  421.5 35.5 %collective-permute-start.38 = (bf16[6400,128]{1,0:T(8,128)(2,1)S(1)}, bf16[6400,128]{1,0:T(8,128)(2,1)S(1)}, u32[]{:S(2)}, u32[]{:S(2)}) collective-permute-start(bf16[6400,128]{1,0:T(8,128)(2,1)S(1)} %get-tuple-element.288.refs_3_), channel_id=1, source_target_pairs={{4,0},{5,1},{6,2},{7,3},{0,4},{1,5},{2,6},{3,7},{12,8},{13,9},{14,... | collective-permute-start | bytes 4915208 | tf_op jit(solution)/shard_map/ppermute | solution.py:543
  476.1 27.2 %collective-permute-start.45 = (f32[1600,128]{1,0:T(8,128)S(1)}, f32[1600,128]{1,0:T(8,128)S(1)}, u32[]{:S(2)}, u32[]{:S(2)}) collective-permute-start(f32[1600,128]{1,0:T(8,128)S(1)} %get-tuple-element.286.refs_4_), channel_id=1, source_target_pairs={{0,4},{1,5},{2,6},{3,7},{4,0},{5,1},{6,2},{7,3},{8,12},{9,13},{10,... | collective-permute-start | bytes 2457608 | tf_op jit(solution)/shard_map/ppermute | solution.py:549
  477.2 43.7 %collective-permute-start.44 = (f32[1600,128]{1,0:T(8,128)S(1)}, f32[1600,128]{1,0:T(8,128)S(1)}, u32[]{:S(2)}, u32[]{:S(2)}) collective-permute-start(f32[1600,128]{1,0:T(8,128)S(1)} %get-tuple-element.287.refs_5_), channel_id=1, source_target_pairs={{0,4},{1,5},{2,6},{3,7},{4,0},{5,1},{6,2},{7,3},{8,12},{9,13},{10,... | collective-permute-start | bytes 2457608 | tf_op jit(solution)/shard_map/ppermute | solution.py:549
  479.0 48.7 %collective-permute-start.41 = (f32[552,128]{1,0:T(8,128)S(1)}, f32[552,128]{1,0:T(8,128)S(1)}, u32[]{:S(2)}, u32[]{:S(2)}) collective-permute-start(f32[552,128]{1,0:T(8,128)S(1)} %get-tuple-element.294), channel_id=1, source_target_pairs={{0,2},{1,3},{2,0},{3,1},{4,6},{5,7},{6,4},{7,5},{8,10},{9,11},{10,... | collective-permute-start | bytes 847880 | tf_op jit(solution)/shard_map/ppermute | solution.py:563
  479.4 48.3 %collective-permute-start.42 = (f32[552,128]{1,0:T(8,128)S(1)}, f32[552,128]{1,0:T(8,128)S(1)}, u32[]{:S(2)}, u32[]{:S(2)}) collective-permute-start(f32[552,128]{1,0:T(8,128)S(1)} %get-tuple-element.295), channel_id=1, source_target_pairs={{0,4},{1,5},{2,6},{3,7},{4,0},{5,1},{6,2},{7,3},{8,12},{9,13},{10,... | collective-permute-start | bytes 847880 | tf_op jit(solution)/shard_map/ppermute | solution.py:563
  480.4 47.3 %collective-permute-start.43 = (f32[552,128]{1,0:T(8,128)S(1)}, f32[552,128]{1,0:T(8,128)S(1)}, u32[]{:S(2)}, u32[]{:S(2)}) collective-permute-start(f32[552,128]{1,0:T(8,128)S(1)} %get-tuple-element.296), channel_id=1, source_target_pairs={{0,6},{1,7},{2,4},{3,5},{4,2},{5,3},{6,0},{7,1},{8,14},{9,15},{10,... | collective-permute-start | bytes 847880 | tf_op jit(solution)/shard_map/ppermute | solution.py:563
  527.8 21.3 %collective-permute-start.46 = (f32[552,128]{1,0:T(8,128)S(1)}, f32[552,128]{1,0:T(8,128)S(1)}, u32[]{:S(2)}, u32[]{:S(2)}) collective-permute-start(f32[552,128]{1,0:T(8,128)S(1)} %get-tuple-element.300.refs_0_), channel_id=1, source_target_pairs={{0,2},{1,3},{2,0},{3,1},{4,6},{5,7},{6,4},{7,5},{8,10},{9,11},{10,... | collective-permute-start | bytes 847880 | tf_op jit(solution)/shard_map/ppermute | solution.py:567
  528.1 20.9 %collective-permute-start.47 = (f32[552,128]{1,0:T(8,128)S(1)}, f32[552,128]{1,0:T(8,128)S(1)}, u32[]{:S(2)}, u32[]{:S(2)}) collective-permute-start(f32[552,128]{1,0:T(8,128)S(1)} %get-tuple-element.300.refs_0_), channel_id=1, source_target_pairs={{0,4},{1,5},{2,6},{3,7},{4,0},{5,1},{6,2},{7,3},{8,12},{9,13},{10,... | collective-permute-start | bytes 847880 | tf_op jit(solution)/shard_map/ppermute | solution.py:567
  529.2 19.9 %collective-permute-start.48 = (f32[552,128]{1,0:T(8,128)S(1)}, f32[552,128]{1,0:T(8,128)S(1)}, u32[]{:S(2)}, u32[]{:S(2)}) collective-permute-start(f32[552,128]{1,0:T(8,128)S(1)} %get-tuple-element.300.refs_0_), channel_id=1, source_target_pairs={{0,6},{1,7},{2,4},{3,5},{4,2},{5,3},{6,0},{7,1},{8,14},{9,15},{10,... | collective-permute-start | bytes 847880 | tf_op jit(solution)/shard_map/ppermute | solution.py:567
  553.1 37.5 %collective-permute-start.49 = (bf16[6400,128]{1,0:T(8,128)(2,1)S(1)}, bf16[6400,128]{1,0:T(8,128)(2,1)S(1)}, u32[]{:S(2)}, u32[]{:S(2)}) collective-permute-start(bf16[6400,128]{1,0:T(8,128)(2,1)S(1)} %get-tuple-element.305.refs_3_), channel_id=1, source_target_pairs={{5,0},{6,1},{7,2},{0,3},{1,4},{2,5},{3,6},{4,7},{13,8},{14,9},{15,... | collective-permute-start | bytes 4915208 | tf_op jit(solution)/shard_map/ppermute | solution.py:543
  610.7 25.5 %collective-permute-start.55 = (f32[1600,128]{1,0:T(8,128)S(1)}, f32[1600,128]{1,0:T(8,128)S(1)}, u32[]{:S(2)}, u32[]{:S(2)}) collective-permute-start(f32[1600,128]{1,0:T(8,128)S(1)} %get-tuple-element.311.refs_5_), channel_id=1, source_target_pairs={{0,5},{1,6},{2,7},{3,0},{4,1},{5,2},{6,3},{7,4},{8,13},{9,14},{10,... | collective-permute-start | bytes 2457608 | tf_op jit(solution)/shard_map/ppermute | solution.py:549
  612.5 30.6 %collective-permute-start.52 = (f32[552,128]{1,0:T(8,128)S(1)}, f32[552,128]{1,0:T(8,128)S(1)}, u32[]{:S(2)}, u32[]{:S(2)}) collective-permute-start(f32[552,128]{1,0:T(8,128)S(1)} %get-tuple-element.318), channel_id=1, source_target_pairs={{0,2},{1,3},{2,0},{3,1},{4,6},{5,7},{6,4},{7,5},{8,10},{9,11},{10,... | collective-permute-start | bytes 847880 | tf_op jit(solution)/shard_map/ppermute | solution.py:563
  612.6 30.5 %collective-permute-start.53 = (f32[552,128]{1,0:T(8,128)S(1)}, f32[552,128]{1,0:T(8,128)S(1)}, u32[]{:S(2)}, u32[]{:S(2)}) collective-permute-start(f32[552,128]{1,0:T(8,128)S(1)} %get-tuple-element.319), channel_id=1, source_target_pairs={{0,4},{1,5},{2,6},{3,7},{4,0},{5,1},{6,2},{7,3},{8,12},{9,13},{10,... | collective-permute-start | bytes 847880 | tf_op jit(solution)/shard_map/ppermute | solution.py:563
  613.6 29.5 %collective-permute-start.54 = (f32[552,128]{1,0:T(8,128)S(1)}, f32[552,128]{1,0:T(8,128)S(1)}, u32[]{:S(2)}, u32[]{:S(2)}) collective-permute-start(f32[552,128]{1,0:T(8,128)S(1)} %get-tuple-element.320), channel_id=1, source_target_pairs={{0,6},{1,7},{2,4},{3,5},{4,2},{5,3},{6,0},{7,1},{8,14},{9,15},{10,... | collective-permute-start | bytes 847880 | tf_op jit(solution)/shard_map/ppermute | solution.py:563
  643.1 30.4 %collective-permute-start.57 = (f32[552,128]{1,0:T(8,128)S(1)}, f32[552,128]{1,0:T(8,128)S(1)}, u32[]{:S(2)}, u32[]{:S(2)}) collective-permute-start(f32[552,128]{1,0:T(8,128)S(1)} %get-tuple-element.324.refs_0_), channel_id=1, source_target_pairs={{0,2},{1,3},{2,0},{3,1},{4,6},{5,7},{6,4},{7,5},{8,10},{9,11},{10,... | collective-permute-start | bytes 847880 | tf_op jit(solution)/shard_map/ppermute | solution.py:567
  654.3 19.3 %collective-permute-start.58 = (f32[552,128]{1,0:T(8,128)S(1)}, f32[552,128]{1,0:T(8,128)S(1)}, u32[]{:S(2)}, u32[]{:S(2)}) collective-permute-start(f32[552,128]{1,0:T(8,128)S(1)} %get-tuple-element.324.refs_0_), channel_id=1, source_target_pairs={{0,4},{1,5},{2,6},{3,7},{4,0},{5,1},{6,2},{7,3},{8,12},{9,13},{10,... | collective-permute-start | bytes 847880 | tf_op jit(solution)/shard_map/ppermute | solution.py:567
  677.6 39.4 %collective-permute-start.60 = (bf16[6400,128]{1,0:T(8,128)(2,1)S(1)}, bf16[6400,128]{1,0:T(8,128)(2,1)S(1)}, u32[]{:S(2)}, u32[]{:S(2)}) collective-permute-start(bf16[6400,128]{1,0:T(8,128)(2,1)S(1)} %get-tuple-element.332.refs_3_), channel_id=1, source_target_pairs={{6,0},{7,1},{0,2},{1,3},{2,4},{3,5},{4,6},{5,7},{14,8},{15,9},{8,1... | collective-permute-start | bytes 4915208 | tf_op jit(solution)/shard_map/ppermute | solution.py:543
  736.0 21.2 %collective-permute-start.67 = (f32[1600,128]{1,0:T(8,128)S(1)}, f32[1600,128]{1,0:T(8,128)S(1)}, u32[]{:S(2)}, u32[]{:S(2)}) collective-permute-start(f32[1600,128]{1,0:T(8,128)S(1)} %get-tuple-element.330.refs_4_), channel_id=1, source_target_pairs={{0,6},{1,7},{2,0},{3,1},{4,2},{5,3},{6,4},{7,5},{8,14},{9,15},{10,... | collective-permute-start | bytes 2457608 | tf_op jit(solution)/shard_map/ppermute | solution.py:549
  737.2 37.4 %collective-permute-start.66 = (f32[1600,128]{1,0:T(8,128)S(1)}, f32[1600,128]{1,0:T(8,128)S(1)}, u32[]{:S(2)}, u32[]{:S(2)}) collective-permute-start(f32[1600,128]{1,0:T(8,128)S(1)} %get-tuple-element.331.refs_5_), channel_id=1, source_target_pairs={{0,6},{1,7},{2,0},{3,1},{4,2},{5,3},{6,4},{7,5},{8,14},{9,15},{10,... | collective-permute-start | bytes 2457608 | tf_op jit(solution)/shard_map/ppermute | solution.py:549
  738.8 42.6 %collective-permute-start.63 = (f32[552,128]{1,0:T(8,128)S(1)}, f32[552,128]{1,0:T(8,128)S(1)}, u32[]{:S(2)}, u32[]{:S(2)}) collective-permute-start(f32[552,128]{1,0:T(8,128)S(1)} %get-tuple-element.338), channel_id=1, source_target_pairs={{0,2},{1,3},{2,0},{3,1},{4,6},{5,7},{6,4},{7,5},{8,10},{9,11},{10,... | collective-permute-start | bytes 847880 | tf_op jit(solution)/shard_map/ppermute | solution.py:563
  739.7 41.8 %collective-permute-start.64 = (f32[552,128]{1,0:T(8,128)S(1)}, f32[552,128]{1,0:T(8,128)S(1)}, u32[]{:S(2)}, u32[]{:S(2)}) collective-permute-start(f32[552,128]{1,0:T(8,128)S(1)} %get-tuple-element.339), channel_id=1, source_target_pairs={{0,4},{1,5},{2,6},{3,7},{4,0},{5,1},{6,2},{7,3},{8,12},{9,13},{10,... | collective-permute-start | bytes 847880 | tf_op jit(solution)/shard_map/ppermute | solution.py:563
  740.7 46.0 %collective-permute-start.65 = (f32[552,128]{1,0:T(8,128)S(1)}, f32[552,128]{1,0:T(8,128)S(1)}, u32[]{:S(2)}, u32[]{:S(2)}) collective-permute-start(f32[552,128]{1,0:T(8,128)S(1)} %get-tuple-element.340), channel_id=1, source_target_pairs={{0,6},{1,7},{2,4},{3,5},{4,2},{5,3},{6,0},{7,1},{8,14},{9,15},{10,... | collective-permute-start | bytes 847880 | tf_op jit(solution)/shard_map/ppermute | solution.py:563
  786.8 21.5 %collective-permute-start.68 = (f32[552,128]{1,0:T(8,128)S(1)}, f32[552,128]{1,0:T(8,128)S(1)}, u32[]{:S(2)}, u32[]{:S(2)}) collective-permute-start(f32[552,128]{1,0:T(8,128)S(1)} %get-tuple-element.344.refs_0_), channel_id=1, source_target_pairs={{0,2},{1,3},{2,0},{3,1},{4,6},{5,7},{6,4},{7,5},{8,10},{9,11},{10,... | collective-permute-start | bytes 847880 | tf_op jit(solution)/shard_map/ppermute | solution.py:567
  788.1 20.2 %collective-permute-start.69 = (f32[552,128]{1,0:T(8,128)S(1)}, f32[552,128]{1,0:T(8,128)S(1)}, u32[]{:S(2)}, u32[]{:S(2)}) collective-permute-start(f32[552,128]{1,0:T(8,128)S(1)} %get-tuple-element.344.refs_0_), channel_id=1, source_target_pairs={{0,4},{1,5},{2,6},{3,7},{4,0},{5,1},{6,2},{7,3},{8,12},{9,13},{10,... | collective-permute-start | bytes 847880 | tf_op jit(solution)/shard_map/ppermute | solution.py:567
  (34 other events, 349.1 us)
Sparse Core Ops, SparseCore 0:
  16.1 5.0 sort.23.cloned.1.call-done
  24.5 11.4 sort.21.cloned.1.call-done
  (2 shorter events, 0.0 us)

commit v2 on v1

--- a/solution.py
+++ b/solution.py
@@ -17,6 +17,7 @@
 LANES = 128
 MIB = 1 << 20
 GRANT = 7
+STEP = 16
 TAILS_FIRST = (True, False)
 
 VM = pl.BlockSpec(memory_space=pltpu.VMEM)
@@ -82,6 +83,17 @@
         return carry
 
     return lax.fori_loop(0, count // unroll, step, carry)
+
+
+def run_sums(acc, grads, same):
+    sums = []
+    for u in range(0, len(grads), 2):
+        first, second = same[u], same[u + 1]
+        sums.append(acc * first + grads[u])
+        both = jnp.full(acc.shape, first, F32) * second
+        acc = acc * both + (grads[u] * second + grads[u + 1])
+        sums.append(acc)
+    return acc, sums
 
 
 def copy_rows(idx_ref, count, src, dst, skip=0):
@@ -245,13 +257,17 @@
     def chunk(c, acc):
         base = c * size
 
-        def collect(base, at, u, acc):
-            acc = acc * same_ref[base + u] + grad_ref[plan_ref[base + u]]
-            sum_ref[at + u] = acc
-            row_ref[at + u] = tab_ref[plan_ref[base + (count + u)]]
+        def collect(b, acc):
+            at = b * STEP
+            src = base + at
+            grads = [grad_ref[plan_ref[src + u]] for u in range(STEP)]
+            acc, sums = run_sums(acc, grads, [same_ref[src + u] for u in range(STEP)])
+            for u in range(STEP):
+                sum_ref[at + u] = sums[u]
+                row_ref[at + u] = tab_ref[plan_ref[src + (count + u)]]
             return acc
 
-        acc = each(size, collect, acc, base)
+        acc = lax.fori_loop(0, size // STEP, collect, acc)
 
         def update(b, carry):
             at = b * (block * 4)
@@ -358,12 +374,15 @@
     sum_ref = grad_out.at[pl.ds(2 * edges, rel_rows)]
     sum_ref[...] = jnp.zeros(sum_ref.shape, F32)
 
-    def scatter(base, at, u, acc):
-        acc = acc * same_ref[base + u] + hold_ref[plan_ref[base + u]]
-        sum_ref[plan_ref[base + (edges + u)]] = acc
+    def scatter(b, acc):
+        at = b * STEP
+        grads = [hold_ref[plan_ref[at + u]] for u in range(STEP)]
+        acc, sums = run_sums(acc, grads, [same_ref[at + u] for u in range(STEP)])
+        for u in range(STEP):
+            sum_ref[plan_ref[at + (edges + u)]] = sums[u]
         return acc
 
-    each(edges, scatter, jnp.zeros((4, LANES), F32))
+    lax.fori_loop(0, edges // STEP, scatter, jnp.zeros((4, LANES), F32))
     drel_out = flat(tab_ref.at[pl.ds(*areas['drel'])])
     pack_rows(drel_out, flat(sum_ref), rel_rows, 0, 8, None)
     used, half = rel_rows * 25 // 8, give_out.shape[0]

time: 853 us -> 846 us (level)
  no operation moved by 1% of the time
where the time goes in v2:
time: 846 us; the launch traced here: 836 us
  Pallas kernels  377 us (45%)
  waiting for transfers between devices  314 us (37%)
  starting transfers between devices  100 us (12%)
  local copies, waits for them, and re-layouts  21.6 us (3%)
  between operations  15.5 us (2%)
    pallas_call x61, Pallas kernels, call(): pl.pallas_call(body, in_specs=in_specs + [VM], out_specs=[VM] + out_specs...  341 us
    ppermute x6, waiting for transfers between devices, train(): far_tails = lax.ppermute(tails, 'ent', to_asker)  156 us
    ppermute x12, waiting for transfers between devices, train(): far_heads.append(lax.ppermute(heads[side], 'ent', to_owner))  138 us
    ppermute x18, starting transfers between devices, train(): totals = [lax.ppermute(total, 'ent', away(2 * hop + 2)) for hop in range(3)]  30.3 us
    ppermute x12, starting transfers between devices, train(): far_heads.append(lax.ppermute(heads[side], 'ent', to_owner))  29.6 us
    ppermute x18, starting transfers between devices, train(): lax.ppermute(x, 'ent', away(2 * hop + 2))  21.1 us
    pallas_call x1, Pallas kernels, train(): pl.pallas_call(store_kernel, grid=(part_rows // cols,), in_specs=[VM], ou...  19.5 us
  transfers between devices with their start and end apart: 72, of which 31 were waited for; matrix products, arithmetic and copies ran while one was open for 1% of the time, Pallas kernels for 25%

profile of v2, /device:TPU:0, one launch (start us, length us, event | category | flops | bytes accessed | tf_op | source)
XLA Modules:
  0.0 835.7 jit_solution(645962172149064857)
XLA Ops:
  25.2 11.0 %sort.17.cloned.1.call-done = s32[6,3072]{1,0:T(8,128)} async-done(((s32[6,3072]{1,0:T(8,128)}), s32[6,3072]{1,0:T(8,128)}) %sort.17.cloned.1.call-update) | async-done | bytes 73744 | tf_op jit(solution)/shard_map/sort | solution.py:509
  38.5 14.5 %load.1.refs_2_ = f32[22360,4,128]{2,1,0:T(4,128)S(1)} custom-call(f32[400,16384]{1,0:T(8,128)} %bitcast.164), custom_call_target="tpu_custom_call" | custom-call | tf_op jit(solution)/shard_map/load/pallas_call | solution.py:552
  53.1 5.1 shard_map.111.refs_2_
  67.0 16.4 %collective-permute-done.6.refs_6_ = bf16[6400,128]{1,0:T(8,128)(2,1)S(1)} collective-permute-done((bf16[6400,128]{1,0:T(8,128)(2,1)S(1)}, bf16[6400,128]{1,0:T(8,128)(2,1)S(1)}, u32[]{:S(2)}, u32[]{:S(2)}) %collective-permute-start.6) | collective-permute-done | bytes 1638432 | tf_op jit(solution)/shard_map/ppermute | solution.py:562
  84.6 16.4 %shard_map.114 = (f32[22360,4,128]{2,1,0:T(4,128)S(1)}, f32[2208,128]{1,0:T(8,128)S(1)}) custom-call(s32[1024]{0:T(1024)S(1)} %bitcast.144, s32[2048]{0:T(1024)S(1)} %bitcast.133, f32[1024]{0:T(1024)S(1)} %bitcast.163, f32[1024,8]{1,0:T(8,128)S(1)} %pad_bitcast_fusion.refs_3_, ...), custom_call_target="tpu_custom_call", output_to_operand_aliasing={{0}: (7, {})} | custom-call | tf_op jit(solution)/shard_map/pallas_call | solution.py:547
  107.7 12.3 %collective-permute-done.12.refs_2_ = f32[1600,128]{1,0:T(8,128)S(1)} collective-permute-done((f32[1600,128]{1,0:T(8,128)S(1)}, f32[1600,128]{1,0:T(8,128)S(1)}, u32[]{:S(2)}, u32[]{:S(2)}) %collective-permute-start.12) | collective-permute-done | bytes 819232 | tf_op jit(solution)/shard_map/ppermute | solution.py:568
  120.0 6.6 shard_map.116.refs_4_
  129.1 7.1 shard_map.117.refs_4_
  139.9 17.9 %shard_map.119.refs_4_ = f32[22360,4,128]{2,1,0:T(4,128)S(1)} custom-call(s32[9216]{0:T(1024)S(1)} %bitcast.108, f32[3072]{0:T(1024)S(1)} %bitcast.115, f32[22360,4,128]{2,1,0:T(4,128)S(1)} %get-tuple-element.239.refs_2_), custom_call_target="tpu_custom_call", output_to_operand_aliasing={{}: (2, {})} | custom-call | tf_op jit(solution)/shard_map/pallas_call | solution.py:547
  167.9 29.7 %collective-permute-done.16.refs_6_ = bf16[6400,128]{1,0:T(8,128)(2,1)S(1)} collective-permute-done((bf16[6400,128]{1,0:T(8,128)(2,1)S(1)}, bf16[6400,128]{1,0:T(8,128)(2,1)S(1)}, u32[]{:S(2)}, u32[]{:S(2)}) %collective-permute-start.16) | collective-permute-done | bytes 1638432 | tf_op jit(solution)/shard_map/ppermute | solution.py:562
  198.8 16.4 %shard_map.124 = (f32[22360,4,128]{2,1,0:T(4,128)S(1)}, f32[2208,128]{1,0:T(8,128)S(1)}) custom-call(s32[1024]{0:T(1024)S(1)} %bitcast.142, s32[2048]{0:T(1024)S(1)} %bitcast.132, f32[1024]{0:T(1024)S(1)} %bitcast.162, f32[1024,8]{1,0:T(8,128)S(1)} %pad_bitcast_fusion.refs_3_, ...), custom_call_target="tpu_custom_call", output_to_operand_aliasing={{0}: (7, {})} | custom-call | tf_op jit(solution)/shard_map/pallas_call | solution.py:547
  222.1 15.4 %collective-permute-done.23.refs_2_ = f32[1600,128]{1,0:T(8,128)S(1)} collective-permute-done((f32[1600,128]{1,0:T(8,128)S(1)}, f32[1600,128]{1,0:T(8,128)S(1)}, u32[]{:S(2)}, u32[]{:S(2)}) %collective-permute-start.23) | collective-permute-done | bytes 819232 | tf_op jit(solution)/shard_map/ppermute | solution.py:568
  237.5 6.6 shard_map.126.refs_4_
  244.1 10.9 %collective-permute-done.22.refs_2_ = f32[1600,128]{1,0:T(8,128)S(1)} collective-permute-done((f32[1600,128]{1,0:T(8,128)S(1)}, f32[1600,128]{1,0:T(8,128)S(1)}, u32[]{:S(2)}, u32[]{:S(2)}) %collective-permute-start.22) | collective-permute-done | bytes 819232 | tf_op jit(solution)/shard_map/ppermute | solution.py:568
  255.0 6.9 shard_map.127.refs_4_
  261.9 4.7 collective-permute-done.21.refs_3_
  270.2 17.9 %shard_map.129.refs_4_ = f32[22360,4,128]{2,1,0:T(4,128)S(1)} custom-call(s32[9216]{0:T(1024)S(1)} %bitcast.107, f32[3072]{0:T(1024)S(1)} %bitcast.114, f32[22360,4,128]{2,1,0:T(4,128)S(1)} %get-tuple-element.259.refs_2_), custom_call_target="tpu_custom_call", output_to_operand_aliasing={{}: (2, {})} | custom-call | tf_op jit(solution)/shard_map/pallas_call | solution.py:547
  298.1 14.6 %collective-permute-done.27.refs_6_ = bf16[6400,128]{1,0:T(8,128)(2,1)S(1)} collective-permute-done((bf16[6400,128]{1,0:T(8,128)(2,1)S(1)}, bf16[6400,128]{1,0:T(8,128)(2,1)S(1)}, u32[]{:S(2)}, u32[]{:S(2)}) %collective-permute-start.27) | collective-permute-done | bytes 1638432 | tf_op jit(solution)/shard_map/ppermute | solution.py:562
  313.9 16.4 %shard_map.134 = (f32[22360,4,128]{2,1,0:T(4,128)S(1)}, f32[2208,128]{1,0:T(8,128)S(1)}) custom-call(s32[1024]{0:T(1024)S(1)} %bitcast.140, s32[2048]{0:T(1024)S(1)} %bitcast.131, f32[1024]{0:T(1024)S(1)} %bitcast.161, f32[1024,8]{1,0:T(8,128)S(1)} %pad_bitcast_fusion.refs_3_, ...), custom_call_target="tpu_custom_call", output_to_operand_aliasing={{0}: (7, {})} | custom-call | tf_op jit(solution)/shard_map/pallas_call | solution.py:547
  330.5 17.8 %collective-permute-start.34 = (f32[1600,128]{1,0:T(8,128)S(1)}, f32[1600,128]{1,0:T(8,128)S(1)}, u32[]{:S(2)}, u32[]{:S(2)}) collective-permute-start(f32[1600,128]{1,0:T(8,128)S(1)} %get-tuple-element.266.refs_4_), channel_id=1, source_target_pairs={{0,3},{1,4},{2,5},{3,6},{4,7},{5,0},{6,1},{7,2},{8,11},{9,12},{10,... | collective-permute-start | bytes 2457608 | tf_op jit(solution)/shard_map/ppermute | solution.py:568
  353.1 11.1 %collective-permute-done.34.refs_2_ = f32[1600,128]{1,0:T(8,128)S(1)} collective-permute-done((f32[1600,128]{1,0:T(8,128)S(1)}, f32[1600,128]{1,0:T(8,128)S(1)}, u32[]{:S(2)}, u32[]{:S(2)}) %collective-permute-start.34) | collective-permute-done | bytes 819232 | tf_op jit(solution)/shard_map/ppermute | solution.py:568
  364.2 6.8 shard_map.136.refs_4_
  371.1 15.0 %collective-permute-done.33.refs_2_ = f32[1600,128]{1,0:T(8,128)S(1)} collective-permute-done((f32[1600,128]{1,0:T(8,128)S(1)}, f32[1600,128]{1,0:T(8,128)S(1)}, u32[]{:S(2)}, u32[]{:S(2)}) %collective-permute-start.33) | collective-permute-done | bytes 819232 | tf_op jit(solution)/shard_map/ppermute | solution.py:568
  386.1 6.8 shard_map.137.refs_4_
  396.5 17.9 %shard_map.139.refs_4_ = f32[22360,4,128]{2,1,0:T(4,128)S(1)} custom-call(s32[9216]{0:T(1024)S(1)} %bitcast.106, f32[3072]{0:T(1024)S(1)} %bitcast.113, f32[22360,4,128]{2,1,0:T(4,128)S(1)} %get-tuple-element.283.refs_2_), custom_call_target="tpu_custom_call", output_to_operand_aliasing={{}: (2, {})} | custom-call | tf_op jit(solution)/shard_map/pallas_call | solution.py:547
  423.8 30.1 %collective-permute-done.38.refs_6_ = bf16[6400,128]{1,0:T(8,128)(2,1)S(1)} collective-permute-done((bf16[6400,128]{1,0:T(8,128)(2,1)S(1)}, bf16[6400,128]{1,0:T(8,128)(2,1)S(1)}, u32[]{:S(2)}, u32[]{:S(2)}) %collective-permute-start.38) | collective-permute-done | bytes 1638432 | tf_op jit(solution)/shard_map/ppermute | solution.py:562
  455.1 16.9 %shard_map.144 = (f32[22360,4,128]{2,1,0:T(4,128)S(1)}, f32[2208,128]{1,0:T(8,128)S(1)}) custom-call(s32[1024]{0:T(1024)S(1)} %bitcast.138, s32[2048]{0:T(1024)S(1)} %bitcast.130, f32[1024]{0:T(1024)S(1)} %bitcast.160, f32[1024,8]{1,0:T(8,128)S(1)} %pad_bitcast_fusion.refs_3_, ...), custom_call_target="tpu_custom_call", output_to_operand_aliasing={{0}: (7, {})} | custom-call | tf_op jit(solution)/shard_map/pallas_call | solution.py:547
  478.4 20.8 %collective-permute-done.45.refs_2_ = f32[1600,128]{1,0:T(8,128)S(1)} collective-permute-done((f32[1600,128]{1,0:T(8,128)S(1)}, f32[1600,128]{1,0:T(8,128)S(1)}, u32[]{:S(2)}, u32[]{:S(2)}) %collective-permute-start.45) | collective-permute-done | bytes 819232 | tf_op jit(solution)/shard_map/ppermute | solution.py:568
  499.2 6.6 shard_map.146.refs_4_
  505.8 10.9 %collective-permute-done.44.refs_2_ = f32[1600,128]{1,0:T(8,128)S(1)} collective-permute-done((f32[1600,128]{1,0:T(8,128)S(1)}, f32[1600,128]{1,0:T(8,128)S(1)}, u32[]{:S(2)}, u32[]{:S(2)}) %collective-permute-start.44) | collective-permute-done | bytes 819232 | tf_op jit(solution)/shard_map/ppermute | solution.py:568
  516.8 6.8 shard_map.147.refs_4_
  527.2 17.9 %shard_map.149.refs_4_ = f32[22360,4,128]{2,1,0:T(4,128)S(1)} custom-call(s32[9216]{0:T(1024)S(1)} %bitcast.105, f32[3072]{0:T(1024)S(1)} %bitcast.112, f32[22360,4,128]{2,1,0:T(4,128)S(1)} %get-tuple-element.303.refs_2_), custom_call_target="tpu_custom_call", output_to_operand_aliasing={{}: (2, {})} | custom-call | tf_op jit(solution)/shard_map/pallas_call | solution.py:547
  554.3 32.3 %collective-permute-done.49.refs_6_ = bf16[6400,128]{1,0:T(8,128)(2,1)S(1)} collective-permute-done((bf16[6400,128]{1,0:T(8,128)(2,1)S(1)}, bf16[6400,128]{1,0:T(8,128)(2,1)S(1)}, u32[]{:S(2)}, u32[]{:S(2)}) %collective-permute-start.49) | collective-permute-done | bytes 1638432 | tf_op jit(solution)/shard_map/ppermute | solution.py:562
  587.8 16.6 %shard_map.154 = (f32[22360,4,128]{2,1,0:T(4,128)S(1)}, f32[2208,128]{1,0:T(8,128)S(1)}) custom-call(s32[1024]{0:T(1024)S(1)} %bitcast.136, s32[2048]{0:T(1024)S(1)} %bitcast.129, f32[1024]{0:T(1024)S(1)} %bitcast.159, f32[1024,8]{1,0:T(8,128)S(1)} %pad_bitcast_fusion.refs_3_, ...), custom_call_target="tpu_custom_call", output_to_operand_aliasing={{0}: (7, {})} | custom-call | tf_op jit(solution)/shard_map/pallas_call | solution.py:547
  610.8 10.7 %collective-permute-done.56.refs_2_ = f32[1600,128]{1,0:T(8,128)S(1)} collective-permute-done((f32[1600,128]{1,0:T(8,128)S(1)}, f32[1600,128]{1,0:T(8,128)S(1)}, u32[]{:S(2)}, u32[]{:S(2)}) %collective-permute-start.56) | collective-permute-done | bytes 819232 | tf_op jit(solution)/shard_map/ppermute | solution.py:568
  621.6 6.6 shard_map.156.refs_4_
  631.1 6.8 shard_map.157.refs_4_
  638.0 11.2 %collective-permute-start.57 = (f32[552,128]{1,0:T(8,128)S(1)}, f32[552,128]{1,0:T(8,128)S(1)}, u32[]{:S(2)}, u32[]{:S(2)}) collective-permute-start(f32[552,128]{1,0:T(8,128)S(1)} %get-tuple-element.324.refs_0_), channel_id=1, source_target_pairs={{0,2},{1,3},{2,0},{3,1},{4,6},{5,7},{6,4},{7,5},{8,10},{9,11},{10,... | collective-permute-start | bytes 847880 | tf_op jit(solution)/shard_map/ppermute | solution.py:586
  650.6 17.9 %shard_map.159.refs_4_ = f32[22360,4,128]{2,1,0:T(4,128)S(1)} custom-call(s32[9216]{0:T(1024)S(1)} %bitcast.104, f32[3072]{0:T(1024)S(1)} %bitcast.111, f32[22360,4,128]{2,1,0:T(4,128)S(1)} %get-tuple-element.327.refs_2_), custom_call_target="tpu_custom_call", output_to_operand_aliasing={{}: (2, {})} | custom-call | tf_op jit(solution)/shard_map/pallas_call | solution.py:547
  679.0 33.0 %collective-permute-done.60.refs_6_ = bf16[6400,128]{1,0:T(8,128)(2,1)S(1)} collective-permute-done((bf16[6400,128]{1,0:T(8,128)(2,1)S(1)}, bf16[6400,128]{1,0:T(8,128)(2,1)S(1)}, u32[]{:S(2)}, u32[]{:S(2)}) %collective-permute-start.60) | collective-permute-done | bytes 1638432 | tf_op jit(solution)/shard_map/ppermute | solution.py:562
  713.1 16.6 %shard_map.164 = (f32[22360,4,128]{2,1,0:T(4,128)S(1)}, f32[2208,128]{1,0:T(8,128)S(1)}) custom-call(s32[1024]{0:T(1024)S(1)} %bitcast.134, s32[2048]{0:T(1024)S(1)} %bitcast.128, f32[1024]{0:T(1024)S(1)} %bitcast.158, f32[1024,8]{1,0:T(8,128)S(1)} %pad_bitcast_fusion.refs_3_, ...), custom_call_target="tpu_custom_call", output_to_operand_aliasing={{0}: (7, {})} | custom-call | tf_op jit(solution)/shard_map/pallas_call | solution.py:547
  736.2 14.8 %collective-permute-done.67.refs_2_ = f32[1600,128]{1,0:T(8,128)S(1)} collective-permute-done((f32[1600,128]{1,0:T(8,128)S(1)}, f32[1600,128]{1,0:T(8,128)S(1)}, u32[]{:S(2)}, u32[]{:S(2)}) %collective-permute-start.67) | collective-permute-done | bytes 819232 | tf_op jit(solution)/shard_map/ppermute | solution.py:568
  751.0 6.6 shard_map.166.refs_4_
  757.6 10.9 %collective-permute-done.66.refs_2_ = f32[1600,128]{1,0:T(8,128)S(1)} collective-permute-done((f32[1600,128]{1,0:T(8,128)S(1)}, f32[1600,128]{1,0:T(8,128)S(1)}, u32[]{:S(2)}, u32[]{:S(2)}) %collective-permute-start.66) | collective-permute-done | bytes 819232 | tf_op jit(solution)/shard_map/ppermute | solution.py:568
  768.5 6.8 shard_map.167.refs_4_
  775.3 5.2 collective-permute-done.65.refs_3_
  784.1 18.1 %shard_map.169.refs_4_ = f32[22360,4,128]{2,1,0:T(4,128)S(1)} custom-call(s32[9216]{0:T(1024)S(1)} %bitcast.103, f32[3072]{0:T(1024)S(1)} %bitcast.110, f32[22360,4,128]{2,1,0:T(4,128)S(1)} %get-tuple-element.347.refs_2_), custom_call_target="tpu_custom_call", output_to_operand_aliasing={{}: (2, {})} | custom-call | tf_op jit(solution)/shard_map/pallas_call | solution.py:547
  806.8 19.5 %store.1 = (f32[400,16384]{1,0:T(8,128)}, f32[1,16384]{1,0:T(1,128)}) custom-call(f32[22360,4,128]{2,1,0:T(4,128)S(1)} %shard_map.171.tab_ref), custom_call_target="tpu_custom_call" | custom-call | tf_op jit(solution)/shard_map/store/pallas_call | solution.py:592
  (223 shorter events, 154.5 us)
Async XLA Ops:
  62.1 21.3 %collective-permute-start.6 = (bf16[6400,128]{1,0:T(8,128)(2,1)S(1)}, bf16[6400,128]{1,0:T(8,128)(2,1)S(1)}, u32[]{:S(2)}, u32[]{:S(2)}) collective-permute-start(bf16[6400,128]{1,0:T(8,128)(2,1)S(1)} %get-tuple-element.218.refs_3_), channel_id=1, source_target_pairs={{1,0},{2,1},{3,2},{4,3},{5,4},{6,5},{7,6},{0,7},{9,8},{10,9},{11,1... | collective-permute-start | bytes 4915208 | tf_op jit(solution)/shard_map/ppermute | solution.py:562
  101.7 27.5 %collective-permute-start.11 = (f32[1600,128]{1,0:T(8,128)S(1)}, f32[1600,128]{1,0:T(8,128)S(1)}, u32[]{:S(2)}, u32[]{:S(2)}) collective-permute-start(f32[1600,128]{1,0:T(8,128)S(1)} %get-tuple-element.224.refs_5_), channel_id=1, source_target_pairs={{0,1},{1,2},{2,3},{3,4},{4,5},{5,6},{6,7},{7,0},{8,9},{9,10},{10,1... | collective-permute-start | bytes 2457608 | tf_op jit(solution)/shard_map/ppermute | solution.py:568
  104.1 32.2 %collective-permute-start.10 = (f32[552,128]{1,0:T(8,128)S(1)}, f32[552,128]{1,0:T(8,128)S(1)}, u32[]{:S(2)}, u32[]{:S(2)}) collective-permute-start(f32[552,128]{1,0:T(8,128)S(1)} %get-tuple-element.232), channel_id=1, source_target_pairs={{0,6},{1,7},{2,4},{3,5},{4,2},{5,3},{6,0},{7,1},{8,14},{9,15},{10,... | collective-permute-start | bytes 847880 | tf_op jit(solution)/shard_map/ppermute | solution.py:582
  106.8 29.5 %collective-permute-start.8 = (f32[552,128]{1,0:T(8,128)S(1)}, f32[552,128]{1,0:T(8,128)S(1)}, u32[]{:S(2)}, u32[]{:S(2)}) collective-permute-start(f32[552,128]{1,0:T(8,128)S(1)} %get-tuple-element.230), channel_id=1, source_target_pairs={{0,2},{1,3},{2,0},{3,1},{4,6},{5,7},{6,4},{7,5},{8,10},{9,11},{10,... | collective-permute-start | bytes 847880 | tf_op jit(solution)/shard_map/ppermute | solution.py:582
  107.3 29.0 %collective-permute-start.9 = (f32[552,128]{1,0:T(8,128)S(1)}, f32[552,128]{1,0:T(8,128)S(1)}, u32[]{:S(2)}, u32[]{:S(2)}) collective-permute-start(f32[552,128]{1,0:T(8,128)S(1)} %get-tuple-element.231), channel_id=1, source_target_pairs={{0,4},{1,5},{2,6},{3,7},{4,0},{5,1},{6,2},{7,3},{8,12},{9,13},{10,... | collective-permute-start | bytes 847880 | tf_op jit(solution)/shard_map/ppermute | solution.py:582
  136.4 21.4 %collective-permute-start.13 = (f32[552,128]{1,0:T(8,128)S(1)}, f32[552,128]{1,0:T(8,128)S(1)}, u32[]{:S(2)}, u32[]{:S(2)}) collective-permute-start(f32[552,128]{1,0:T(8,128)S(1)} %get-tuple-element.236.refs_0_), channel_id=1, source_target_pairs={{0,2},{1,3},{2,0},{3,1},{4,6},{5,7},{6,4},{7,5},{8,10},{9,11},{10,... | collective-permute-start | bytes 847880 | tf_op jit(solution)/shard_map/ppermute | solution.py:586
  137.2 20.6 %collective-permute-start.14 = (f32[552,128]{1,0:T(8,128)S(1)}, f32[552,128]{1,0:T(8,128)S(1)}, u32[]{:S(2)}, u32[]{:S(2)}) collective-permute-start(f32[552,128]{1,0:T(8,128)S(1)} %get-tuple-element.236.refs_0_), channel_id=1, source_target_pairs={{0,4},{1,5},{2,6},{3,7},{4,0},{5,1},{6,2},{7,3},{8,12},{9,13},{10,... | collective-permute-start | bytes 847880 | tf_op jit(solution)/shard_map/ppermute | solution.py:586
  161.8 35.9 %collective-permute-start.16 = (bf16[6400,128]{1,0:T(8,128)(2,1)S(1)}, bf16[6400,128]{1,0:T(8,128)(2,1)S(1)}, u32[]{:S(2)}, u32[]{:S(2)}) collective-permute-start(bf16[6400,128]{1,0:T(8,128)(2,1)S(1)} %get-tuple-element.244.refs_3_), channel_id=1, source_target_pairs={{2,0},{3,1},{4,2},{5,3},{6,4},{7,5},{0,6},{1,7},{10,8},{11,9},{12,... | collective-permute-start | bytes 4915208 | tf_op jit(solution)/shard_map/ppermute | solution.py:562
  215.3 22.2 %collective-permute-start.23 = (f32[1600,128]{1,0:T(8,128)S(1)}, f32[1600,128]{1,0:T(8,128)S(1)}, u32[]{:S(2)}, u32[]{:S(2)}) collective-permute-start(f32[1600,128]{1,0:T(8,128)S(1)} %get-tuple-element.242.refs_4_), channel_id=1, source_target_pairs={{0,2},{1,3},{2,4},{3,5},{4,6},{5,7},{6,0},{7,1},{8,10},{9,11},{10,... | collective-permute-start | bytes 2457608 | tf_op jit(solution)/shard_map/ppermute | solution.py:568
  217.2 37.8 %collective-permute-start.22 = (f32[1600,128]{1,0:T(8,128)S(1)}, f32[1600,128]{1,0:T(8,128)S(1)}, u32[]{:S(2)}, u32[]{:S(2)}) collective-permute-start(f32[1600,128]{1,0:T(8,128)S(1)} %get-tuple-element.243.refs_5_), channel_id=1, source_target_pairs={{0,2},{1,3},{2,4},{3,5},{4,6},{5,7},{6,0},{7,1},{8,10},{9,11},{10,... | collective-permute-start | bytes 2457608 | tf_op jit(solution)/shard_map/ppermute | solution.py:568
  218.6 43.4 %collective-permute-start.19 = (f32[552,128]{1,0:T(8,128)S(1)}, f32[552,128]{1,0:T(8,128)S(1)}, u32[]{:S(2)}, u32[]{:S(2)}) collective-permute-start(f32[552,128]{1,0:T(8,128)S(1)} %get-tuple-element.250), channel_id=1, source_target_pairs={{0,2},{1,3},{2,0},{3,1},{4,6},{5,7},{6,4},{7,5},{8,10},{9,11},{10,... | collective-permute-start | bytes 847880 | tf_op jit(solution)/shard_map/ppermute | solution.py:582
  220.1 41.8 %collective-permute-start.20 = (f32[552,128]{1,0:T(8,128)S(1)}, f32[552,128]{1,0:T(8,128)S(1)}, u32[]{:S(2)}, u32[]{:S(2)}) collective-permute-start(f32[552,128]{1,0:T(8,128)S(1)} %get-tuple-element.251), channel_id=1, source_target_pairs={{0,4},{1,5},{2,6},{3,7},{4,0},{5,1},{6,2},{7,3},{8,12},{9,13},{10,... | collective-permute-start | bytes 847880 | tf_op jit(solution)/shard_map/ppermute | solution.py:582
  221.2 45.4 %collective-permute-start.21 = (f32[552,128]{1,0:T(8,128)S(1)}, f32[552,128]{1,0:T(8,128)S(1)}, u32[]{:S(2)}, u32[]{:S(2)}) collective-permute-start(f32[552,128]{1,0:T(8,128)S(1)} %get-tuple-element.252), channel_id=1, source_target_pairs={{0,6},{1,7},{2,4},{3,5},{4,2},{5,3},{6,0},{7,1},{8,14},{9,15},{10,... | collective-permute-start | bytes 847880 | tf_op jit(solution)/shard_map/ppermute | solution.py:582
  266.7 21.4 %collective-permute-start.24 = (f32[552,128]{1,0:T(8,128)S(1)}, f32[552,128]{1,0:T(8,128)S(1)}, u32[]{:S(2)}, u32[]{:S(2)}) collective-permute-start(f32[552,128]{1,0:T(8,128)S(1)} %get-tuple-element.256.refs_0_), channel_id=1, source_target_pairs={{0,2},{1,3},{2,0},{3,1},{4,6},{5,7},{6,4},{7,5},{8,10},{9,11},{10,... | collective-permute-start | bytes 847880 | tf_op jit(solution)/shard_map/ppermute | solution.py:586
  268.1 20.0 %collective-permute-start.25 = (f32[552,128]{1,0:T(8,128)S(1)}, f32[552,128]{1,0:T(8,128)S(1)}, u32[]{:S(2)}, u32[]{:S(2)}) collective-permute-start(f32[552,128]{1,0:T(8,128)S(1)} %get-tuple-element.256.refs_0_), channel_id=1, source_target_pairs={{0,4},{1,5},{2,6},{3,7},{4,0},{5,1},{6,2},{7,3},{8,12},{9,13},{10,... | collective-permute-start | bytes 847880 | tf_op jit(solution)/shard_map/ppermute | solution.py:586
  292.1 20.6 %collective-permute-start.27 = (bf16[6400,128]{1,0:T(8,128)(2,1)S(1)}, bf16[6400,128]{1,0:T(8,128)(2,1)S(1)}, u32[]{:S(2)}, u32[]{:S(2)}) collective-permute-start(bf16[6400,128]{1,0:T(8,128)(2,1)S(1)} %get-tuple-element.261.refs_3_), channel_id=1, source_target_pairs={{3,0},{4,1},{5,2},{6,3},{7,4},{0,5},{1,6},{2,7},{11,8},{12,9},{13,... | collective-permute-start | bytes 4915208 | tf_op jit(solution)/shard_map/ppermute | solution.py:562
  330.5 33.8 %collective-permute-start.34 = (f32[1600,128]{1,0:T(8,128)S(1)}, f32[1600,128]{1,0:T(8,128)S(1)}, u32[]{:S(2)}, u32[]{:S(2)}) collective-permute-start(f32[1600,128]{1,0:T(8,128)S(1)} %get-tuple-element.266.refs_4_), channel_id=1, source_target_pairs={{0,3},{1,4},{2,5},{3,6},{4,7},{5,0},{6,1},{7,2},{8,11},{9,12},{10,... | collective-permute-start | bytes 2457608 | tf_op jit(solution)/shard_map/ppermute | solution.py:568
  348.3 37.8 %collective-permute-start.33 = (f32[1600,128]{1,0:T(8,128)S(1)}, f32[1600,128]{1,0:T(8,128)S(1)}, u32[]{:S(2)}, u32[]{:S(2)}) collective-permute-start(f32[1600,128]{1,0:T(8,128)S(1)} %get-tuple-element.267.refs_5_), channel_id=1, source_target_pairs={{0,3},{1,4},{2,5},{3,6},{4,7},{5,0},{6,1},{7,2},{8,11},{9,12},{10,... | collective-permute-start | bytes 2457608 | tf_op jit(solution)/shard_map/ppermute | solution.py:568
  349.5 43.3 %collective-permute-start.30 = (f32[552,128]{1,0:T(8,128)S(1)}, f32[552,128]{1,0:T(8,128)S(1)}, u32[]{:S(2)}, u32[]{:S(2)}) collective-permute-start(f32[552,128]{1,0:T(8,128)S(1)} %get-tuple-element.274), channel_id=1, source_target_pairs={{0,2},{1,3},{2,0},{3,1},{4,6},{5,7},{6,4},{7,5},{8,10},{9,11},{10,... | collective-permute-start | bytes 847880 | tf_op jit(solution)/shard_map/ppermute | solution.py:582
  351.2 41.7 %collective-permute-start.31 = (f32[552,128]{1,0:T(8,128)S(1)}, f32[552,128]{1,0:T(8,128)S(1)}, u32[]{:S(2)}, u32[]{:S(2)}) collective-permute-start(f32[552,128]{1,0:T(8,128)S(1)} %get-tuple-element.275), channel_id=1, source_target_pairs={{0,4},{1,5},{2,6},{3,7},{4,0},{5,1},{6,2},{7,3},{8,12},{9,13},{10,... | collective-permute-start | bytes 847880 | tf_op jit(solution)/shard_map/ppermute | solution.py:582
  352.3 40.6 %collective-permute-start.32 = (f32[552,128]{1,0:T(8,128)S(1)}, f32[552,128]{1,0:T(8,128)S(1)}, u32[]{:S(2)}, u32[]{:S(2)}) collective-permute-start(f32[552,128]{1,0:T(8,128)S(1)} %get-tuple-element.276), channel_id=1, source_target_pairs={{0,6},{1,7},{2,4},{3,5},{4,2},{5,3},{6,0},{7,1},{8,14},{9,15},{10,... | collective-permute-start | bytes 847880 | tf_op jit(solution)/shard_map/ppermute | solution.py:582
  393.0 21.4 %collective-permute-start.35 = (f32[552,128]{1,0:T(8,128)S(1)}, f32[552,128]{1,0:T(8,128)S(1)}, u32[]{:S(2)}, u32[]{:S(2)}) collective-permute-start(f32[552,128]{1,0:T(8,128)S(1)} %get-tuple-element.280.refs_0_), channel_id=1, source_target_pairs={{0,2},{1,3},{2,0},{3,1},{4,6},{5,7},{6,4},{7,5},{8,10},{9,11},{10,... | collective-permute-start | bytes 847880 | tf_op jit(solution)/shard_map/ppermute | solution.py:586
  393.0 21.3 %collective-permute-start.36 = (f32[552,128]{1,0:T(8,128)S(1)}, f32[552,128]{1,0:T(8,128)S(1)}, u32[]{:S(2)}, u32[]{:S(2)}) collective-permute-start(f32[552,128]{1,0:T(8,128)S(1)} %get-tuple-element.280.refs_0_), channel_id=1, source_target_pairs={{0,4},{1,5},{2,6},{3,7},{4,0},{5,1},{6,2},{7,3},{8,12},{9,13},{10,... | collective-permute-start | bytes 847880 | tf_op jit(solution)/shard_map/ppermute | solution.py:586
  394.0 20.4 %collective-permute-start.37 = (f32[552,128]{1,0:T(8,128)S(1)}, f32[552,128]{1,0:T(8,128)S(1)}, u32[]{:S(2)}, u32[]{:S(2)}) collective-permute-start(f32[552,128]{1,0:T(8,128)S(1)} %get-tuple-element.280.refs_0_), channel_id=1, source_target_pairs={{0,6},{1,7},{2,4},{3,5},{4,2},{5,3},{6,0},{7,1},{8,14},{9,15},{10,... | collective-permute-start | bytes 847880 | tf_op jit(solution)/shard_map/ppermute | solution.py:586
  418.4 35.5 %collective-permute-start.38 = (bf16[6400,128]{1,0:T(8,128)(2,1)S(1)}, bf16[6400,128]{1,0:T(8,128)(2,1)S(1)}, u32[]{:S(2)}, u32[]{:S(2)}) collective-permute-start(bf16[6400,128]{1,0:T(8,128)(2,1)S(1)} %get-tuple-element.288.refs_3_), channel_id=1, source_target_pairs={{4,0},{5,1},{6,2},{7,3},{0,4},{1,5},{2,6},{3,7},{12,8},{13,9},{14,... | collective-permute-start | bytes 4915208 | tf_op jit(solution)/shard_map/ppermute | solution.py:562
  472.0 27.2 %collective-permute-start.45 = (f32[1600,128]{1,0:T(8,128)S(1)}, f32[1600,128]{1,0:T(8,128)S(1)}, u32[]{:S(2)}, u32[]{:S(2)}) collective-permute-start(f32[1600,128]{1,0:T(8,128)S(1)} %get-tuple-element.286.refs_4_), channel_id=1, source_target_pairs={{0,4},{1,5},{2,6},{3,7},{4,0},{5,1},{6,2},{7,3},{8,12},{9,13},{10,... | collective-permute-start | bytes 2457608 | tf_op jit(solution)/shard_map/ppermute | solution.py:568
  473.1 43.7 %collective-permute-start.44 = (f32[1600,128]{1,0:T(8,128)S(1)}, f32[1600,128]{1,0:T(8,128)S(1)}, u32[]{:S(2)}, u32[]{:S(2)}) collective-permute-start(f32[1600,128]{1,0:T(8,128)S(1)} %get-tuple-element.287.refs_5_), channel_id=1, source_target_pairs={{0,4},{1,5},{2,6},{3,7},{4,0},{5,1},{6,2},{7,3},{8,12},{9,13},{10,... | collective-permute-start | bytes 2457608 | tf_op jit(solution)/shard_map/ppermute | solution.py:568
  474.9 48.7 %collective-permute-start.41 = (f32[552,128]{1,0:T(8,128)S(1)}, f32[552,128]{1,0:T(8,128)S(1)}, u32[]{:S(2)}, u32[]{:S(2)}) collective-permute-start(f32[552,128]{1,0:T(8,128)S(1)} %get-tuple-element.294), channel_id=1, source_target_pairs={{0,2},{1,3},{2,0},{3,1},{4,6},{5,7},{6,4},{7,5},{8,10},{9,11},{10,... | collective-permute-start | bytes 847880 | tf_op jit(solution)/shard_map/ppermute | solution.py:582
  475.2 48.3 %collective-permute-start.42 = (f32[552,128]{1,0:T(8,128)S(1)}, f32[552,128]{1,0:T(8,128)S(1)}, u32[]{:S(2)}, u32[]{:S(2)}) collective-permute-start(f32[552,128]{1,0:T(8,128)S(1)} %get-tuple-element.295), channel_id=1, source_target_pairs={{0,4},{1,5},{2,6},{3,7},{4,0},{5,1},{6,2},{7,3},{8,12},{9,13},{10,... | collective-permute-start | bytes 847880 | tf_op jit(solution)/shard_map/ppermute | solution.py:582
  476.3 47.3 %collective-permute-start.43 = (f32[552,128]{1,0:T(8,128)S(1)}, f32[552,128]{1,0:T(8,128)S(1)}, u32[]{:S(2)}, u32[]{:S(2)}) collective-permute-start(f32[552,128]{1,0:T(8,128)S(1)} %get-tuple-element.296), channel_id=1, source_target_pairs={{0,6},{1,7},{2,4},{3,5},{4,2},{5,3},{6,0},{7,1},{8,14},{9,15},{10,... | collective-permute-start | bytes 847880 | tf_op jit(solution)/shard_map/ppermute | solution.py:582
  523.7 21.4 %collective-permute-start.46 = (f32[552,128]{1,0:T(8,128)S(1)}, f32[552,128]{1,0:T(8,128)S(1)}, u32[]{:S(2)}, u32[]{:S(2)}) collective-permute-start(f32[552,128]{1,0:T(8,128)S(1)} %get-tuple-element.300.refs_0_), channel_id=1, source_target_pairs={{0,2},{1,3},{2,0},{3,1},{4,6},{5,7},{6,4},{7,5},{8,10},{9,11},{10,... | collective-permute-start | bytes 847880 | tf_op jit(solution)/shard_map/ppermute | solution.py:586
  524.0 21.1 %collective-permute-start.47 = (f32[552,128]{1,0:T(8,128)S(1)}, f32[552,128]{1,0:T(8,128)S(1)}, u32[]{:S(2)}, u32[]{:S(2)}) collective-permute-start(f32[552,128]{1,0:T(8,128)S(1)} %get-tuple-element.300.refs_0_), channel_id=1, source_target_pairs={{0,4},{1,5},{2,6},{3,7},{4,0},{5,1},{6,2},{7,3},{8,12},{9,13},{10,... | collective-permute-start | bytes 847880 | tf_op jit(solution)/shard_map/ppermute | solution.py:586
  525.1 20.0 %collective-permute-start.48 = (f32[552,128]{1,0:T(8,128)S(1)}, f32[552,128]{1,0:T(8,128)S(1)}, u32[]{:S(2)}, u32[]{:S(2)}) collective-permute-start(f32[552,128]{1,0:T(8,128)S(1)} %get-tuple-element.300.refs_0_), channel_id=1, source_target_pairs={{0,6},{1,7},{2,4},{3,5},{4,2},{5,3},{6,0},{7,1},{8,14},{9,15},{10,... | collective-permute-start | bytes 847880 | tf_op jit(solution)/shard_map/ppermute | solution.py:586
  549.1 37.5 %collective-permute-start.49 = (bf16[6400,128]{1,0:T(8,128)(2,1)S(1)}, bf16[6400,128]{1,0:T(8,128)(2,1)S(1)}, u32[]{:S(2)}, u32[]{:S(2)}) collective-permute-start(bf16[6400,128]{1,0:T(8,128)(2,1)S(1)} %get-tuple-element.305.refs_3_), channel_id=1, source_target_pairs={{5,0},{6,1},{7,2},{0,3},{1,4},{2,5},{3,6},{4,7},{13,8},{14,9},{15,... | collective-permute-start | bytes 4915208 | tf_op jit(solution)/shard_map/ppermute | solution.py:562
  605.6 25.5 %collective-permute-start.55 = (f32[1600,128]{1,0:T(8,128)S(1)}, f32[1600,128]{1,0:T(8,128)S(1)}, u32[]{:S(2)}, u32[]{:S(2)}) collective-permute-start(f32[1600,128]{1,0:T(8,128)S(1)} %get-tuple-element.311.refs_5_), channel_id=1, source_target_pairs={{0,5},{1,6},{2,7},{3,0},{4,1},{5,2},{6,3},{7,4},{8,13},{9,14},{10,... | collective-permute-start | bytes 2457608 | tf_op jit(solution)/shard_map/ppermute | solution.py:568
  607.3 30.5 %collective-permute-start.52 = (f32[552,128]{1,0:T(8,128)S(1)}, f32[552,128]{1,0:T(8,128)S(1)}, u32[]{:S(2)}, u32[]{:S(2)}) collective-permute-start(f32[552,128]{1,0:T(8,128)S(1)} %get-tuple-element.318), channel_id=1, source_target_pairs={{0,2},{1,3},{2,0},{3,1},{4,6},{5,7},{6,4},{7,5},{8,10},{9,11},{10,... | collective-permute-start | bytes 847880 | tf_op jit(solution)/shard_map/ppermute | solution.py:582
  607.4 30.5 %collective-permute-start.53 = (f32[552,128]{1,0:T(8,128)S(1)}, f32[552,128]{1,0:T(8,128)S(1)}, u32[]{:S(2)}, u32[]{:S(2)}) collective-permute-start(f32[552,128]{1,0:T(8,128)S(1)} %get-tuple-element.319), channel_id=1, source_target_pairs={{0,4},{1,5},{2,6},{3,7},{4,0},{5,1},{6,2},{7,3},{8,12},{9,13},{10,... | collective-permute-start | bytes 847880 | tf_op jit(solution)/shard_map/ppermute | solution.py:582
  608.4 29.4 %collective-permute-start.54 = (f32[552,128]{1,0:T(8,128)S(1)}, f32[552,128]{1,0:T(8,128)S(1)}, u32[]{:S(2)}, u32[]{:S(2)}) collective-permute-start(f32[552,128]{1,0:T(8,128)S(1)} %get-tuple-element.320), channel_id=1, source_target_pairs={{0,6},{1,7},{2,4},{3,5},{4,2},{5,3},{6,0},{7,1},{8,14},{9,15},{10,... | collective-permute-start | bytes 847880 | tf_op jit(solution)/shard_map/ppermute | solution.py:582
  638.0 30.5 %collective-permute-start.57 = (f32[552,128]{1,0:T(8,128)S(1)}, f32[552,128]{1,0:T(8,128)S(1)}, u32[]{:S(2)}, u32[]{:S(2)}) collective-permute-start(f32[552,128]{1,0:T(8,128)S(1)} %get-tuple-element.324.refs_0_), channel_id=1, source_target_pairs={{0,2},{1,3},{2,0},{3,1},{4,6},{5,7},{6,4},{7,5},{8,10},{9,11},{10,... | collective-permute-start | bytes 847880 | tf_op jit(solution)/shard_map/ppermute | solution.py:586
  649.1 19.4 %collective-permute-start.58 = (f32[552,128]{1,0:T(8,128)S(1)}, f32[552,128]{1,0:T(8,128)S(1)}, u32[]{:S(2)}, u32[]{:S(2)}) collective-permute-start(f32[552,128]{1,0:T(8,128)S(1)} %get-tuple-element.324.refs_0_), channel_id=1, source_target_pairs={{0,4},{1,5},{2,6},{3,7},{4,0},{5,1},{6,2},{7,3},{8,12},{9,13},{10,... | collective-permute-start | bytes 847880 | tf_op jit(solution)/shard_map/ppermute | solution.py:586
  672.6 39.4 %collective-permute-start.60 = (bf16[6400,128]{1,0:T(8,128)(2,1)S(1)}, bf16[6400,128]{1,0:T(8,128)(2,1)S(1)}, u32[]{:S(2)}, u32[]{:S(2)}) collective-permute-start(bf16[6400,128]{1,0:T(8,128)(2,1)S(1)} %get-tuple-element.332.refs_3_), channel_id=1, source_target_pairs={{6,0},{7,1},{0,2},{1,3},{2,4},{3,5},{4,6},{5,7},{14,8},{15,9},{8,1... | collective-permute-start | bytes 4915208 | tf_op jit(solution)/shard_map/ppermute | solution.py:562
  729.8 21.2 %collective-permute-start.67 = (f32[1600,128]{1,0:T(8,128)S(1)}, f32[1600,128]{1,0:T(8,128)S(1)}, u32[]{:S(2)}, u32[]{:S(2)}) collective-permute-start(f32[1600,128]{1,0:T(8,128)S(1)} %get-tuple-element.330.refs_4_), channel_id=1, source_target_pairs={{0,6},{1,7},{2,0},{3,1},{4,2},{5,3},{6,4},{7,5},{8,14},{9,15},{10,... | collective-permute-start | bytes 2457608 | tf_op jit(solution)/shard_map/ppermute | solution.py:568
  731.0 37.5 %collective-permute-start.66 = (f32[1600,128]{1,0:T(8,128)S(1)}, f32[1600,128]{1,0:T(8,128)S(1)}, u32[]{:S(2)}, u32[]{:S(2)}) collective-permute-start(f32[1600,128]{1,0:T(8,128)S(1)} %get-tuple-element.331.refs_5_), channel_id=1, source_target_pairs={{0,6},{1,7},{2,0},{3,1},{4,2},{5,3},{6,4},{7,5},{8,14},{9,15},{10,... | collective-permute-start | bytes 2457608 | tf_op jit(solution)/shard_map/ppermute | solution.py:568
  732.7 42.6 %collective-permute-start.63 = (f32[552,128]{1,0:T(8,128)S(1)}, f32[552,128]{1,0:T(8,128)S(1)}, u32[]{:S(2)}, u32[]{:S(2)}) collective-permute-start(f32[552,128]{1,0:T(8,128)S(1)} %get-tuple-element.338), channel_id=1, source_target_pairs={{0,2},{1,3},{2,0},{3,1},{4,6},{5,7},{6,4},{7,5},{8,10},{9,11},{10,... | collective-permute-start | bytes 847880 | tf_op jit(solution)/shard_map/ppermute | solution.py:582
  733.5 41.8 %collective-permute-start.64 = (f32[552,128]{1,0:T(8,128)S(1)}, f32[552,128]{1,0:T(8,128)S(1)}, u32[]{:S(2)}, u32[]{:S(2)}) collective-permute-start(f32[552,128]{1,0:T(8,128)S(1)} %get-tuple-element.339), channel_id=1, source_target_pairs={{0,4},{1,5},{2,6},{3,7},{4,0},{5,1},{6,2},{7,3},{8,12},{9,13},{10,... | collective-permute-start | bytes 847880 | tf_op jit(solution)/shard_map/ppermute | solution.py:582
  734.5 46.0 %collective-permute-start.65 = (f32[552,128]{1,0:T(8,128)S(1)}, f32[552,128]{1,0:T(8,128)S(1)}, u32[]{:S(2)}, u32[]{:S(2)}) collective-permute-start(f32[552,128]{1,0:T(8,128)S(1)} %get-tuple-element.340), channel_id=1, source_target_pairs={{0,6},{1,7},{2,4},{3,5},{4,2},{5,3},{6,0},{7,1},{8,14},{9,15},{10,... | collective-permute-start | bytes 847880 | tf_op jit(solution)/shard_map/ppermute | solution.py:582
  780.6 21.6 %collective-permute-start.68 = (f32[552,128]{1,0:T(8,128)S(1)}, f32[552,128]{1,0:T(8,128)S(1)}, u32[]{:S(2)}, u32[]{:S(2)}) collective-permute-start(f32[552,128]{1,0:T(8,128)S(1)} %get-tuple-element.344.refs_0_), channel_id=1, source_target_pairs={{0,2},{1,3},{2,0},{3,1},{4,6},{5,7},{6,4},{7,5},{8,10},{9,11},{10,... | collective-permute-start | bytes 847880 | tf_op jit(solution)/shard_map/ppermute | solution.py:586
  782.0 20.3 %collective-permute-start.69 = (f32[552,128]{1,0:T(8,128)S(1)}, f32[552,128]{1,0:T(8,128)S(1)}, u32[]{:S(2)}, u32[]{:S(2)}) collective-permute-start(f32[552,128]{1,0:T(8,128)S(1)} %get-tuple-element.344.refs_0_), channel_id=1, source_target_pairs={{0,4},{1,5},{2,6},{3,7},{4,0},{5,1},{6,2},{7,3},{8,12},{9,13},{10,... | collective-permute-start | bytes 847880 | tf_op jit(solution)/shard_map/ppermute | solution.py:586
  (34 other events, 349.4 us)
Sparse Core Ops, SparseCore 0:
  16.1 5.0 sort.23.cloned.1.call-done
  24.5 11.4 sort.21.cloned.1.call-done
  (2 shorter events, 0.0 us)
